TPU v7x, 128 devices: a whole 4x4x4 slice. The times are simulated.
128 devices in a mesh: seq: 32 (over y_lo, z, x), head: 4 (over y_hi, core).
Axes of the slice: x: 4, y: 4 (y_hi: 2, y_lo: 2; y = y_hi * 2 + y_lo), z: 4, core: 2. Of those that a mesh axis runs over, the one named last changes fastest.
Arguments:
- queries: bfloat16 [4096, 3072], P('seq', 'head'), may hold values from -8 to 8
- latents: bfloat16 [4096, 576], P('seq'), may hold values from -8 to 8
- key_up: bfloat16 [512, 2048], P(None, 'head'), may hold values from -0.25 to 0.25
- value_up: bfloat16 [512, 2048], P(None, 'head'), may hold values from -0.25 to 0.25
- out_grad: bfloat16 [4096, 2048], P('seq', 'head'), may hold values from -48 to 48
- positions: int32 [4096], P('seq'), may hold values from 0 to 4095, as said below
Outputs:
- query_grad: bfloat16 [4096, 3072], P('seq', 'head')
- latent_grad: float32 [4096, 576], P('seq')
- key_up_grad: float32 [512, 2048], P(None, 'head')
- value_up_grad: float32 [512, 2048], P(None, 'head')
Inputs may be any that keep to these rules, and one draw needn't show every extreme that they name: Every position from 0 to 4095 occurs once; positions come in stripes of 128 consecutive positions in ascending order, each stripe whole within the rows of one device.
All inputs are finite; a program needn't handle non-finite values.
Results may differ from a plain program's by a relative error of at most 0.0084.
Values may be sent and summed in bfloat16 or wider, within the bound.
A program may use at most 64 MiB of HBM per device.

v0:
```python
import math
import jax
import jax.numpy as jnp
from jax import lax
from jax.sharding import PartitionSpec as P

D_LAT = 512
D_ROPE = 64
D_NOPE = 128
D_V = 128
NEG = -1e30


def joined_along(tiles, dim):
    tiles = jnp.moveaxis(tiles, 0, dim)
    dims = tiles.shape
    return tiles.reshape(*dims[:dim], dims[dim] * dims[dim + 1], *dims[dim + 2 :])


def from_everyone(shard, axis):
    size = lax.axis_size(axis)
    return lax.all_to_all(
        jnp.broadcast_to(shard[None], (size, *shard.shape)), axis, 0, 0, tiled=True
    )


def collect(shard, axis, dim):
    return joined_along(from_everyone(shard, axis), dim)


def shifted(value, axis, steps):
    count = lax.axis_size(axis)
    pairs = [(source, (source + steps) % count) for source in range(count)]
    return lax.ppermute(value, axis, pairs)


def taken_together(shard, axis):
    return from_everyone(shard, axis).sum(axis=0)


def cut_along(shard, dim, size):
    before, after = (shard.shape[:dim], shard.shape[dim + 1 :])
    return jnp.moveaxis(shard.reshape(*before, size, -1, *after), dim, 0)


def summed_on_arrival(shard, axis, dim):
    tiles = cut_along(shard, dim, lax.axis_size(axis))
    arrived = lax.all_to_all(tiles, axis, split_axis=0, concat_axis=0, tiled=True)
    return arrived.sum(axis=0)


def filled_up(lines, size):
    spare = -len(lines) % size
    return jnp.pad(lines, [(0, spare)] + [(0, 0)] * (lines.ndim - 1))


def sum_by_parts(shard, axes):
    own = summed_on_arrival(filled_up(shard, lax.axis_size(axes)), axes, 0)
    whole = collect(own, axes, 0)
    return whole[: len(shard)].reshape(shard.shape)


def together(arrays, axis):
    vector, at, done = (jnp.concatenate([a.reshape(-1) for a in arrays]), 0, [])
    so_far = sum_by_parts(vector, axis)
    for a in arrays:
        done.append(so_far[at : at + a.size].reshape(a.shape))
        at += a.size
    return tuple(done)


def up_project(block, key_up, value_up):
    compressed = block[:, :D_LAT]
    key_nope = jnp.dot(compressed, key_up, preferred_element_type=jnp.float32).astype(jnp.bfloat16)
    values = jnp.dot(compressed, value_up, preferred_element_type=jnp.float32).astype(jnp.bfloat16)
    return (key_nope, block[:, D_LAT:], values)


def split_heads(queries, out_grad, key_nope, values):
    heads = key_nope.shape[1] // D_NOPE
    shaped = queries.reshape(queries.shape[0], heads, D_NOPE + D_ROPE)
    grads = out_grad.reshape(out_grad.shape[0], heads, D_V)
    key3 = key_nope.reshape(key_nope.shape[0], heads, D_NOPE)
    value3 = values.reshape(values.shape[0], heads, D_V)
    return (shaped[:, :, :D_NOPE], shaped[:, :, D_NOPE:], grads, key3, value3)


def scores_of(q_nope, q_rope, key3, rope_keys, query_pos, key_pos):
    scale = 1.0 / math.sqrt(D_NOPE + D_ROPE)
    raw = jnp.einsum("bhd,khd->hbk", q_nope, key3, preferred_element_type=jnp.float32)
    raw = raw + jnp.einsum("bhd,kd->hbk", q_rope, rope_keys, preferred_element_type=jnp.float32)
    visible = (key_pos[None, :] <= query_pos[:, None])[None]
    return (raw * scale, visible)


def forward_update(stats, queries, out_grad, query_pos, key_nope, rope_keys, values, key_pos):
    top, total, weighted = stats
    q_nope, q_rope, grads, key3, value3 = split_heads(queries, out_grad, key_nope, values)
    scores, visible = scores_of(q_nope, q_rope, key3, rope_keys, query_pos, key_pos)
    dprobs = jnp.einsum("bhd,khd->hbk", grads, value3, preferred_element_type=jnp.float32)
    masked = jnp.where(visible, scores, NEG)
    new_top = jnp.maximum(top, jnp.max(masked, axis=2))
    weights = jnp.exp(jnp.where(visible, scores - new_top[:, :, None], NEG))
    fade = jnp.exp(top - new_top)
    total = total * fade + jnp.sum(weights, axis=2)
    weighted = weighted * fade + jnp.sum(weights * dprobs, axis=2)
    return (new_top, total, weighted)


def backward_terms(queries, out_grad, query_pos, lse, delta, key_nope, rope_keys, values, key_pos):
    scale = 1.0 / math.sqrt(D_NOPE + D_ROPE)
    q_nope, q_rope, grads, key3, value3 = split_heads(queries, out_grad, key_nope, values)
    scores, visible = scores_of(q_nope, q_rope, key3, rope_keys, query_pos, key_pos)
    probs = jnp.exp(jnp.where(visible, scores - lse[:, :, None], NEG))
    dprobs = jnp.einsum("bhd,khd->hbk", grads, value3, preferred_element_type=jnp.float32)
    dscore = (probs * (dprobs - delta[:, :, None]) * scale).astype(jnp.bfloat16)
    probs16 = probs.astype(jnp.bfloat16)
    grad_nope = jnp.einsum("hbk,khd->bhd", dscore, key3, preferred_element_type=jnp.float32)
    grad_rope = jnp.einsum("hbk,kd->bhd", dscore, rope_keys, preferred_element_type=jnp.float32)
    q_grad = jnp.concatenate([grad_nope, grad_rope], axis=2).reshape(queries.shape[0], -1)
    key_part = jnp.einsum("hbk,bhd->khd", dscore, q_nope, preferred_element_type=jnp.float32)
    value_part = jnp.einsum("hbk,bhd->khd", probs16, grads, preferred_element_type=jnp.float32)
    rope_part = jnp.einsum("hbk,bhd->kd", dscore, q_rope, preferred_element_type=jnp.float32)
    key_rows = key3.shape[0]
    part = jnp.concatenate(
        [key_part.reshape(key_rows, -1), value_part.reshape(key_rows, -1), rope_part], axis=1
    )
    return (q_grad, part)


def shards(queries, latents, key_up, value_up, out_grad, positions):
    rows = queries.shape[0]
    heads = key_up.shape[1] // D_NOPE
    qcols = queries.shape[1]
    nseq = lax.axis_size("seq")
    here = lax.axis_index("seq")
    every_pos = collect(positions, "seq", 0)
    part_width = heads * (D_NOPE + D_V) + D_ROPE

    def owner_start(step):
        return (here - step) % nseq * rows

    def owner_pos(step):
        return lax.dynamic_slice_in_dim(every_pos, owner_start(step), rows, 0)

    start_stats = (
        jnp.full((heads, rows), NEG, jnp.float32),
        jnp.zeros((heads, rows), jnp.float32),
        jnp.zeros((heads, rows), jnp.float32),
    )
    zero_grads = jnp.zeros((rows, part_width), jnp.float32)
    zero_query = jnp.zeros((rows, qcols), jnp.float32)

    def fold_block(stats, block, start):
        key_nope, rope_keys, values = up_project(block, key_up, value_up)
        key_pos = lax.dynamic_slice_in_dim(every_pos, start, block.shape[0], 0)
        return forward_update(
            stats, queries, out_grad, positions, key_nope, rope_keys, values, key_pos
        )

    def grad_block(block, grads, q_acc, step, lse, delta):
        key_nope, rope_keys, values = up_project(block, key_up, value_up)
        q_grad, part = backward_terms(
            queries, out_grad, positions, lse, delta, key_nope, rope_keys, values, owner_pos(step)
        )
        return (grads + part, q_acc + q_grad)

    gathered = lax.all_gather(latents, "seq", axis=0, tiled=True)
    count = gathered.shape[0]
    width = math.gcd(count, 512)

    def turn(index, carry):
        block = lax.dynamic_slice_in_dim(gathered, index * width, width, 0)
        return fold_block(carry, block, index * width)

    top, total, weighted = lax.fori_loop(0, count // width, turn, start_stats)
    lse = top + jnp.log(total)
    delta = weighted / total

    def kept_turn(step, carry):
        grads, q_acc = carry
        block = lax.dynamic_slice_in_dim(gathered, owner_start(step), rows, 0)
        grads, q_acc = grad_block(block, grads, q_acc, step, lse, delta)
        grads = shifted(grads, "seq", 1)
        return (grads, q_acc)

    grads, q_acc = lax.fori_loop(0, nseq - 1, kept_turn, (zero_grads, zero_query))
    last_block = lax.dynamic_slice_in_dim(gathered, owner_start(nseq - 1), rows, 0)
    grads, q_acc = grad_block(last_block, grads, q_acc, nseq - 1, lse, delta)
    key_grads = shifted(grads, "seq", 1)
    split_one = heads * D_NOPE
    split_two = split_one + heads * D_V
    key_grad = key_grads[:, :split_one]
    value_grad = key_grads[:, split_one:split_two]
    key_up32 = key_up.astype(jnp.float32)
    value_up32 = value_up.astype(jnp.float32)
    inner = (((1,), (1,)), ((), ()))
    folded = lax.dot_general(key_grad, key_up32, inner)
    folded = folded + lax.dot_general(value_grad, value_up32, inner)
    latent_part = jnp.concatenate([folded, key_grads[:, split_two:]], axis=1)
    latent_grad = taken_together(latent_part, "head")
    compressed = latents[:, :D_LAT].astype(jnp.float32)
    outer = (((0,), (0,)), ((), ()))
    key_term = lax.dot_general(compressed, key_grad, outer)
    value_term = lax.dot_general(compressed, value_grad, outer)
    key_up_grad, value_up_grad = together((key_term, value_term), "seq")
    return (q_acc.astype(jnp.bfloat16), latent_grad, key_up_grad, value_up_grad)


def solution(mesh):
    in_specs = (
        P("seq", "head"),
        P("seq", None),
        P(None, "head"),
        P(None, "head"),
        P("seq", "head"),
        P("seq"),
    )
    out_specs = (P("seq", "head"), P("seq", None), P(None, "head"), P(None, "head"))
    return jax.shard_map(shards, mesh=mesh, in_specs=in_specs, out_specs=out_specs, check_vma=False)
```

profile of v0, /device:TPU:0, one launch (start us, length us, event | category | flops | bytes accessed | tf_op | source)
XLA Modules:
  0.0 1031.5 jit_solution(13648473115734894433)
XLA Ops:
  9.2 9.4 all-to-all-start
  20.8 6.0 all-to-all-done
  28.9 123.4 %all-gather.2.cloned.1.call-done = bf16[4096,576]{0,1:T(8,128)(2,1)} async-done(((bf16[128,576]{0,1:T(8,128)(2,1)}), bf16[4096,576]{0,1:T(8,128)(2,1)}) %all-gather.2.cloned.1.call-update) | async-done | bytes 4718608 | tf_op jit(solution)/shard_map/all_gather | solution.py:168
  152.4 67.2 %while.36 = (s32[]{:T(128)}, f32[4,128]{1,0:T(4,128)S(1)}, f32[4,128]{1,0:T(4,128)S(1)}, f32[4,128]{1,0:T(4,128)}, s32[4096]{0:T(1024)}, /*index=5*/s32[128]{0:T...) while((s32[]{:T(128)}, f32[4,128]{1,0:T(4,128)S(1)}, ...), condition=%wide.region_4.5_spmd.clone, body=%wide.region_0.4_spmd.clone.sunk | while | flops 708120064 | bytes 10660626 | solution.py:176
  152.4 1.7 convolution_convert_fusion.10
  160.2 1.7 convolution_convert_fusion.10
  163.5 1.7 convolution_convert_fusion.9
  168.7 1.7 convolution_convert_fusion.10
  172.0 1.7 convolution_convert_fusion.9
  177.2 1.7 convolution_convert_fusion.10
  185.7 1.7 convolution_convert_fusion.10
  194.2 1.7 convolution_convert_fusion.10
  202.6 1.7 convolution_convert_fusion.10
  205.9 1.7 convolution_convert_fusion.9
  211.1 1.7 convolution_convert_fusion.10
  214.4 1.7 convolution_convert_fusion.9
  226.1 677.1 %while.37 = (s32[]{:T(128)}, f32[128,1088]{0,1:T(8,128)S(1)}, f32[128,768]{0,1:T(8,128)S(1)}, s32[]{:T(128)}, s32[4096]{0:T(1024)}, /*index=5*/s32[128]{0:T(128)...) while((s32[]{:T(128)}, f32[128,1088]{0,1:T(8,128)S(1)}, ...), condition=%wide.region_6.7_spmd.clone, body=%wide.region_5.6_spmd.clone.sunk | while | flops 244719632 | bytes 11737526 | solution.py:187
  233.8 15.9 %collective-permute-done = f32[128,1088]{0,1:T(8,128)S(1)} collective-permute-done((f32[128,1088]{0,1:T(8,128)}, f32[128,1088]{0,1:T(8,128)S(1)}, u32[]{:S(2)}, u32[]{:S(2)}) %collective-permute-start) | collective-permute-done | bytes 557088 | tf_op jit(solution)/shard_map/while/body/eval_jaxpr/ppermute | solution.py:34
  257.0 15.4 %collective-permute-done = f32[128,1088]{0,1:T(8,128)S(1)} collective-permute-done((f32[128,1088]{0,1:T(8,128)}, f32[128,1088]{0,1:T(8,128)S(1)}, u32[]{:S(2)}, u32[]{:S(2)}) %collective-permute-start) | collective-permute-done | bytes 557088 | tf_op jit(solution)/shard_map/while/body/eval_jaxpr/ppermute | solution.py:34
  279.7 14.5 %collective-permute-done = f32[128,1088]{0,1:T(8,128)S(1)} collective-permute-done((f32[128,1088]{0,1:T(8,128)}, f32[128,1088]{0,1:T(8,128)S(1)}, u32[]{:S(2)}, u32[]{:S(2)}) %collective-permute-start) | collective-permute-done | bytes 557088 | tf_op jit(solution)/shard_map/while/body/eval_jaxpr/ppermute | solution.py:34
  301.6 13.7 %collective-permute-done = f32[128,1088]{0,1:T(8,128)S(1)} collective-permute-done((f32[128,1088]{0,1:T(8,128)}, f32[128,1088]{0,1:T(8,128)S(1)}, u32[]{:S(2)}, u32[]{:S(2)}) %collective-permute-start) | collective-permute-done | bytes 557088 | tf_op jit(solution)/shard_map/while/body/eval_jaxpr/ppermute | solution.py:34
  322.6 12.8 %collective-permute-done = f32[128,1088]{0,1:T(8,128)S(1)} collective-permute-done((f32[128,1088]{0,1:T(8,128)}, f32[128,1088]{0,1:T(8,128)S(1)}, u32[]{:S(2)}, u32[]{:S(2)}) %collective-permute-start) | collective-permute-done | bytes 557088 | tf_op jit(solution)/shard_map/while/body/eval_jaxpr/ppermute | solution.py:34
  342.7 12.8 %collective-permute-done = f32[128,1088]{0,1:T(8,128)S(1)} collective-permute-done((f32[128,1088]{0,1:T(8,128)}, f32[128,1088]{0,1:T(8,128)S(1)}, u32[]{:S(2)}, u32[]{:S(2)}) %collective-permute-start) | collective-permute-done | bytes 557088 | tf_op jit(solution)/shard_map/while/body/eval_jaxpr/ppermute | solution.py:34
  362.8 12.8 %collective-permute-done = f32[128,1088]{0,1:T(8,128)S(1)} collective-permute-done((f32[128,1088]{0,1:T(8,128)}, f32[128,1088]{0,1:T(8,128)S(1)}, u32[]{:S(2)}, u32[]{:S(2)}) %collective-permute-start) | collective-permute-done | bytes 557088 | tf_op jit(solution)/shard_map/while/body/eval_jaxpr/ppermute | solution.py:34
  382.9 12.8 %collective-permute-done = f32[128,1088]{0,1:T(8,128)S(1)} collective-permute-done((f32[128,1088]{0,1:T(8,128)}, f32[128,1088]{0,1:T(8,128)S(1)}, u32[]{:S(2)}, u32[]{:S(2)}) %collective-permute-start) | collective-permute-done | bytes 557088 | tf_op jit(solution)/shard_map/while/body/eval_jaxpr/ppermute | solution.py:34
  403.0 12.8 %collective-permute-done = f32[128,1088]{0,1:T(8,128)S(1)} collective-permute-done((f32[128,1088]{0,1:T(8,128)}, f32[128,1088]{0,1:T(8,128)S(1)}, u32[]{:S(2)}, u32[]{:S(2)}) %collective-permute-start) | collective-permute-done | bytes 557088 | tf_op jit(solution)/shard_map/while/body/eval_jaxpr/ppermute | solution.py:34
  423.1 12.8 %collective-permute-done = f32[128,1088]{0,1:T(8,128)S(1)} collective-permute-done((f32[128,1088]{0,1:T(8,128)}, f32[128,1088]{0,1:T(8,128)S(1)}, u32[]{:S(2)}, u32[]{:S(2)}) %collective-permute-start) | collective-permute-done | bytes 557088 | tf_op jit(solution)/shard_map/while/body/eval_jaxpr/ppermute | solution.py:34
  443.2 12.8 %collective-permute-done = f32[128,1088]{0,1:T(8,128)S(1)} collective-permute-done((f32[128,1088]{0,1:T(8,128)}, f32[128,1088]{0,1:T(8,128)S(1)}, u32[]{:S(2)}, u32[]{:S(2)}) %collective-permute-start) | collective-permute-done | bytes 557088 | tf_op jit(solution)/shard_map/while/body/eval_jaxpr/ppermute | solution.py:34
  463.4 13.4 %collective-permute-done = f32[128,1088]{0,1:T(8,128)S(1)} collective-permute-done((f32[128,1088]{0,1:T(8,128)}, f32[128,1088]{0,1:T(8,128)S(1)}, u32[]{:S(2)}, u32[]{:S(2)}) %collective-permute-start) | collective-permute-done | bytes 557088 | tf_op jit(solution)/shard_map/while/body/eval_jaxpr/ppermute | solution.py:34
  484.0 14.5 %collective-permute-done = f32[128,1088]{0,1:T(8,128)S(1)} collective-permute-done((f32[128,1088]{0,1:T(8,128)}, f32[128,1088]{0,1:T(8,128)S(1)}, u32[]{:S(2)}, u32[]{:S(2)}) %collective-permute-start) | collective-permute-done | bytes 557088 | tf_op jit(solution)/shard_map/while/body/eval_jaxpr/ppermute | solution.py:34
  505.9 15.7 %collective-permute-done = f32[128,1088]{0,1:T(8,128)S(1)} collective-permute-done((f32[128,1088]{0,1:T(8,128)}, f32[128,1088]{0,1:T(8,128)S(1)}, u32[]{:S(2)}, u32[]{:S(2)}) %collective-permute-start) | collective-permute-done | bytes 557088 | tf_op jit(solution)/shard_map/while/body/eval_jaxpr/ppermute | solution.py:34
  528.9 16.8 %collective-permute-done = f32[128,1088]{0,1:T(8,128)S(1)} collective-permute-done((f32[128,1088]{0,1:T(8,128)}, f32[128,1088]{0,1:T(8,128)S(1)}, u32[]{:S(2)}, u32[]{:S(2)}) %collective-permute-start) | collective-permute-done | bytes 557088 | tf_op jit(solution)/shard_map/while/body/eval_jaxpr/ppermute | solution.py:34
  553.0 17.9 %collective-permute-done = f32[128,1088]{0,1:T(8,128)S(1)} collective-permute-done((f32[128,1088]{0,1:T(8,128)}, f32[128,1088]{0,1:T(8,128)S(1)}, u32[]{:S(2)}, u32[]{:S(2)}) %collective-permute-start) | collective-permute-done | bytes 557088 | tf_op jit(solution)/shard_map/while/body/eval_jaxpr/ppermute | solution.py:34
  578.3 18.4 %collective-permute-done = f32[128,1088]{0,1:T(8,128)S(1)} collective-permute-done((f32[128,1088]{0,1:T(8,128)}, f32[128,1088]{0,1:T(8,128)S(1)}, u32[]{:S(2)}, u32[]{:S(2)}) %collective-permute-start) | collective-permute-done | bytes 557088 | tf_op jit(solution)/shard_map/while/body/eval_jaxpr/ppermute | solution.py:34
  604.0 17.6 %collective-permute-done = f32[128,1088]{0,1:T(8,128)S(1)} collective-permute-done((f32[128,1088]{0,1:T(8,128)}, f32[128,1088]{0,1:T(8,128)S(1)}, u32[]{:S(2)}, u32[]{:S(2)}) %collective-permute-start) | collective-permute-done | bytes 557088 | tf_op jit(solution)/shard_map/while/body/eval_jaxpr/ppermute | solution.py:34
  628.9 16.7 %collective-permute-done = f32[128,1088]{0,1:T(8,128)S(1)} collective-permute-done((f32[128,1088]{0,1:T(8,128)}, f32[128,1088]{0,1:T(8,128)S(1)}, u32[]{:S(2)}, u32[]{:S(2)}) %collective-permute-start) | collective-permute-done | bytes 557088 | tf_op jit(solution)/shard_map/while/body/eval_jaxpr/ppermute | solution.py:34
  653.0 15.8 %collective-permute-done = f32[128,1088]{0,1:T(8,128)S(1)} collective-permute-done((f32[128,1088]{0,1:T(8,128)}, f32[128,1088]{0,1:T(8,128)S(1)}, u32[]{:S(2)}, u32[]{:S(2)}) %collective-permute-start) | collective-permute-done | bytes 557088 | tf_op jit(solution)/shard_map/while/body/eval_jaxpr/ppermute | solution.py:34
  676.2 15.0 %collective-permute-done = f32[128,1088]{0,1:T(8,128)S(1)} collective-permute-done((f32[128,1088]{0,1:T(8,128)}, f32[128,1088]{0,1:T(8,128)S(1)}, u32[]{:S(2)}, u32[]{:S(2)}) %collective-permute-start) | collective-permute-done | bytes 557088 | tf_op jit(solution)/shard_map/while/body/eval_jaxpr/ppermute | solution.py:34
  698.5 14.1 %collective-permute-done = f32[128,1088]{0,1:T(8,128)S(1)} collective-permute-done((f32[128,1088]{0,1:T(8,128)}, f32[128,1088]{0,1:T(8,128)S(1)}, u32[]{:S(2)}, u32[]{:S(2)}) %collective-permute-start) | collective-permute-done | bytes 557088 | tf_op jit(solution)/shard_map/while/body/eval_jaxpr/ppermute | solution.py:34
  719.9 13.2 %collective-permute-done = f32[128,1088]{0,1:T(8,128)S(1)} collective-permute-done((f32[128,1088]{0,1:T(8,128)}, f32[128,1088]{0,1:T(8,128)S(1)}, u32[]{:S(2)}, u32[]{:S(2)}) %collective-permute-start) | collective-permute-done | bytes 557088 | tf_op jit(solution)/shard_map/while/body/eval_jaxpr/ppermute | solution.py:34
  740.5 12.8 %collective-permute-done = f32[128,1088]{0,1:T(8,128)S(1)} collective-permute-done((f32[128,1088]{0,1:T(8,128)}, f32[128,1088]{0,1:T(8,128)S(1)}, u32[]{:S(2)}, u32[]{:S(2)}) %collective-permute-start) | collective-permute-done | bytes 557088 | tf_op jit(solution)/shard_map/while/body/eval_jaxpr/ppermute | solution.py:34
  760.6 12.8 %collective-permute-done = f32[128,1088]{0,1:T(8,128)S(1)} collective-permute-done((f32[128,1088]{0,1:T(8,128)}, f32[128,1088]{0,1:T(8,128)S(1)}, u32[]{:S(2)}, u32[]{:S(2)}) %collective-permute-start) | collective-permute-done | bytes 557088 | tf_op jit(solution)/shard_map/while/body/eval_jaxpr/ppermute | solution.py:34
  780.8 12.8 %collective-permute-done = f32[128,1088]{0,1:T(8,128)S(1)} collective-permute-done((f32[128,1088]{0,1:T(8,128)}, f32[128,1088]{0,1:T(8,128)S(1)}, u32[]{:S(2)}, u32[]{:S(2)}) %collective-permute-start) | collective-permute-done | bytes 557088 | tf_op jit(solution)/shard_map/while/body/eval_jaxpr/ppermute | solution.py:34
  800.9 12.8 %collective-permute-done = f32[128,1088]{0,1:T(8,128)S(1)} collective-permute-done((f32[128,1088]{0,1:T(8,128)}, f32[128,1088]{0,1:T(8,128)S(1)}, u32[]{:S(2)}, u32[]{:S(2)}) %collective-permute-start) | collective-permute-done | bytes 557088 | tf_op jit(solution)/shard_map/while/body/eval_jaxpr/ppermute | solution.py:34
  821.0 12.8 %collective-permute-done = f32[128,1088]{0,1:T(8,128)S(1)} collective-permute-done((f32[128,1088]{0,1:T(8,128)}, f32[128,1088]{0,1:T(8,128)S(1)}, u32[]{:S(2)}, u32[]{:S(2)}) %collective-permute-start) | collective-permute-done | bytes 557088 | tf_op jit(solution)/shard_map/while/body/eval_jaxpr/ppermute | solution.py:34
  841.1 18.2 %collective-permute-done = f32[128,1088]{0,1:T(8,128)S(1)} collective-permute-done((f32[128,1088]{0,1:T(8,128)}, f32[128,1088]{0,1:T(8,128)S(1)}, u32[]{:S(2)}, u32[]{:S(2)}) %collective-permute-start) | collective-permute-done | bytes 557088 | tf_op jit(solution)/shard_map/while/body/eval_jaxpr/ppermute | solution.py:34
  866.6 12.8 %collective-permute-done = f32[128,1088]{0,1:T(8,128)S(1)} collective-permute-done((f32[128,1088]{0,1:T(8,128)}, f32[128,1088]{0,1:T(8,128)S(1)}, u32[]{:S(2)}, u32[]{:S(2)}) %collective-permute-start) | collective-permute-done | bytes 557088 | tf_op jit(solution)/shard_map/while/body/eval_jaxpr/ppermute | solution.py:34
  886.8 16.4 %collective-permute-done = f32[128,1088]{0,1:T(8,128)S(1)} collective-permute-done((f32[128,1088]{0,1:T(8,128)}, f32[128,1088]{0,1:T(8,128)S(1)}, u32[]{:S(2)}, u32[]{:S(2)}) %collective-permute-start) | collective-permute-done | bytes 557088 | tf_op jit(solution)/shard_map/while/body/eval_jaxpr/ppermute | solution.py:34
  903.3 13.7 %collective-permute-done.1 = f32[128,1088]{0,1:T(8,128)S(1)} collective-permute-done((f32[128,1088]{0,1:T(8,128)S(1)}, f32[128,1088]{0,1:T(8,128)S(1)}, u32[]{:S(2)}, u32[]{:S(2)}) %collective-permute-start.1) | collective-permute-done | bytes 557088 | tf_op jit(solution)/shard_map/ppermute | solution.py:34
  917.1 2.2 convolution_bitcast_fusion.8
  927.6 3.5 copy.122
  931.2 4.8 all-to-all-start.2
  936.9 17.7 %all-to-all-done.2 = f32[32,1,16384]{2,1,0:T(1,128)} async-done(((f32[32,1,16384]{2,1,0:T(1,128)}), f32[32,1,16384]{2,1,0:T(1,128)}, u32[]{:S(2)}, u32[]{:S(2)}) %all-to-all-start.2) | async-done | bytes 2097184 | tf_op jit(solution)/shard_map/all_to_all | solution.py:48
  955.7 4.5 all-to-all-start.1
  960.1 3.0 reduce_sum.45
  963.1 14.3 %all-to-all-done.1 = f32[4,128,576]{1,2,0:T(8,128)S(1)} async-done(((f32[4,128,576]{1,2,0:T(8,128)}), f32[4,128,576]{1,2,0:T(8,128)S(1)}, u32[]{:S(2)}, u32[]{:S(2)}) %all-to-all-start.1) | async-done | bytes 1179680 | tf_op jit(solution)/shard_map/all_to_all | solution.py:22
  977.5 3.3 broadcast_in_dim.137
  980.7 4.2 all-to-all-start.3
  987.2 1.7 add_convert_fusion
  988.9 2.1 reduce_sum.44
  990.9 22.2 %all-to-all-done.3 = f32[32,1,16384]{2,1,0:T(1,128)S(1)} async-done(((f32[32,1,16384]{2,1,0:T(1,128)}), f32[32,1,16384]{2,1,0:T(1,128)S(1)}, u32[]{:S(2)}, u32[]{:S(2)}) %all-to-all-start.3) | async-done | bytes 2097184 | tf_op jit(solution)/shard_map/all_to_all | solution.py:22
  1013.1 6.8 slice_reduce_fusion
  1019.9 2.4 reshape.262
  1022.3 2.4 reshape.263
  (675 shorter events, 296.4 us)
Async XLA Ops:
  7.2 145.2 %all-gather.2.cloned.1.call-start = ((), (), s32[]{:S(2)}) async-start(), calls=%async_computation.4 | async-start | bytes 4866048 | tf_op jit(solution)/shard_map/all_gather | solution.py:168
  9.2 17.6 %all-to-all-start = ((s32[32,1,128]{2,1,0:T(1,128)}), s32[32,1,128]{2,1,0:T(1,128)}, u32[]{:S(2)}, u32[]{:S(2)}) async-start(s32[32,1,128]{2,1,0:T(1,128)} %broadcast_in_dim.132), calls=%async_computation | async-start | bytes 32768 | tf_op jit(solution)/shard_map/all_to_all | solution.py:22
  152.4 6.6 copy-start.6
  160.2 6.6 copy-start.6
  168.7 6.6 copy-start.6
  177.2 6.6 copy-start.6
  185.7 6.6 copy-start.6
  194.1 6.6 copy-start.6
  202.6 6.5 copy-start.6
  211.1 6.5 copy-start.6
  219.6 6.5 copy-start
  219.6 6.5 copy-start.1
  219.6 6.5 copy-start.7
  221.2 4.6 copy-start.3
  232.3 17.4 %collective-permute-start = (f32[128,1088]{0,1:T(8,128)}, f32[128,1088]{0,1:T(8,128)S(1)}, u32[]{:S(2)}, u32[]{:S(2)}) collective-permute-start(f32[128,1088]{0,1:T(8,128)} %maximum_add_fusion.3), channel_id=1, source_target_pairs={{0,4},{4,8},{8,12},{12,16},{16,20},{20,24},{24,28},{28,32},{32,36}... | collective-permute-start | bytes 1671176 | tf_op jit(solution)/shard_map/while/body/eval_jaxpr/ppermute | solution.py:34
  255.8 16.6 %collective-permute-start = (f32[128,1088]{0,1:T(8,128)}, f32[128,1088]{0,1:T(8,128)S(1)}, u32[]{:S(2)}, u32[]{:S(2)}) collective-permute-start(f32[128,1088]{0,1:T(8,128)} %maximum_add_fusion.3), channel_id=1, source_target_pairs={{0,4},{4,8},{8,12},{12,16},{16,20},{20,24},{24,28},{28,32},{32,36}... | collective-permute-start | bytes 1671176 | tf_op jit(solution)/shard_map/while/body/eval_jaxpr/ppermute | solution.py:34
  278.5 15.7 %collective-permute-start = (f32[128,1088]{0,1:T(8,128)}, f32[128,1088]{0,1:T(8,128)S(1)}, u32[]{:S(2)}, u32[]{:S(2)}) collective-permute-start(f32[128,1088]{0,1:T(8,128)} %maximum_add_fusion.3), channel_id=1, source_target_pairs={{0,4},{4,8},{8,12},{12,16},{16,20},{20,24},{24,28},{28,32},{32,36}... | collective-permute-start | bytes 1671176 | tf_op jit(solution)/shard_map/while/body/eval_jaxpr/ppermute | solution.py:34
  300.4 14.9 %collective-permute-start = (f32[128,1088]{0,1:T(8,128)}, f32[128,1088]{0,1:T(8,128)S(1)}, u32[]{:S(2)}, u32[]{:S(2)}) collective-permute-start(f32[128,1088]{0,1:T(8,128)} %maximum_add_fusion.3), channel_id=1, source_target_pairs={{0,4},{4,8},{8,12},{12,16},{16,20},{20,24},{24,28},{28,32},{32,36}... | collective-permute-start | bytes 1671176 | tf_op jit(solution)/shard_map/while/body/eval_jaxpr/ppermute | solution.py:34
  321.4 14.0 %collective-permute-start = (f32[128,1088]{0,1:T(8,128)}, f32[128,1088]{0,1:T(8,128)S(1)}, u32[]{:S(2)}, u32[]{:S(2)}) collective-permute-start(f32[128,1088]{0,1:T(8,128)} %maximum_add_fusion.3), channel_id=1, source_target_pairs={{0,4},{4,8},{8,12},{12,16},{16,20},{20,24},{24,28},{28,32},{32,36}... | collective-permute-start | bytes 1671176 | tf_op jit(solution)/shard_map/while/body/eval_jaxpr/ppermute | solution.py:34
  341.5 14.0 %collective-permute-start = (f32[128,1088]{0,1:T(8,128)}, f32[128,1088]{0,1:T(8,128)S(1)}, u32[]{:S(2)}, u32[]{:S(2)}) collective-permute-start(f32[128,1088]{0,1:T(8,128)} %maximum_add_fusion.3), channel_id=1, source_target_pairs={{0,4},{4,8},{8,12},{12,16},{16,20},{20,24},{24,28},{28,32},{32,36}... | collective-permute-start | bytes 1671176 | tf_op jit(solution)/shard_map/while/body/eval_jaxpr/ppermute | solution.py:34
  361.6 14.0 %collective-permute-start = (f32[128,1088]{0,1:T(8,128)}, f32[128,1088]{0,1:T(8,128)S(1)}, u32[]{:S(2)}, u32[]{:S(2)}) collective-permute-start(f32[128,1088]{0,1:T(8,128)} %maximum_add_fusion.3), channel_id=1, source_target_pairs={{0,4},{4,8},{8,12},{12,16},{16,20},{20,24},{24,28},{28,32},{32,36}... | collective-permute-start | bytes 1671176 | tf_op jit(solution)/shard_map/while/body/eval_jaxpr/ppermute | solution.py:34
  381.7 14.0 %collective-permute-start = (f32[128,1088]{0,1:T(8,128)}, f32[128,1088]{0,1:T(8,128)S(1)}, u32[]{:S(2)}, u32[]{:S(2)}) collective-permute-start(f32[128,1088]{0,1:T(8,128)} %maximum_add_fusion.3), channel_id=1, source_target_pairs={{0,4},{4,8},{8,12},{12,16},{16,20},{20,24},{24,28},{28,32},{32,36}... | collective-permute-start | bytes 1671176 | tf_op jit(solution)/shard_map/while/body/eval_jaxpr/ppermute | solution.py:34
  401.8 14.0 %collective-permute-start = (f32[128,1088]{0,1:T(8,128)}, f32[128,1088]{0,1:T(8,128)S(1)}, u32[]{:S(2)}, u32[]{:S(2)}) collective-permute-start(f32[128,1088]{0,1:T(8,128)} %maximum_add_fusion.3), channel_id=1, source_target_pairs={{0,4},{4,8},{8,12},{12,16},{16,20},{20,24},{24,28},{28,32},{32,36}... | collective-permute-start | bytes 1671176 | tf_op jit(solution)/shard_map/while/body/eval_jaxpr/ppermute | solution.py:34
  422.0 14.0 %collective-permute-start = (f32[128,1088]{0,1:T(8,128)}, f32[128,1088]{0,1:T(8,128)S(1)}, u32[]{:S(2)}, u32[]{:S(2)}) collective-permute-start(f32[128,1088]{0,1:T(8,128)} %maximum_add_fusion.3), channel_id=1, source_target_pairs={{0,4},{4,8},{8,12},{12,16},{16,20},{20,24},{24,28},{28,32},{32,36}... | collective-permute-start | bytes 1671176 | tf_op jit(solution)/shard_map/while/body/eval_jaxpr/ppermute | solution.py:34
  442.1 14.0 %collective-permute-start = (f32[128,1088]{0,1:T(8,128)}, f32[128,1088]{0,1:T(8,128)S(1)}, u32[]{:S(2)}, u32[]{:S(2)}) collective-permute-start(f32[128,1088]{0,1:T(8,128)} %maximum_add_fusion.3), channel_id=1, source_target_pairs={{0,4},{4,8},{8,12},{12,16},{16,20},{20,24},{24,28},{28,32},{32,36}... | collective-permute-start | bytes 1671176 | tf_op jit(solution)/shard_map/while/body/eval_jaxpr/ppermute | solution.py:34
  462.2 14.5 %collective-permute-start = (f32[128,1088]{0,1:T(8,128)}, f32[128,1088]{0,1:T(8,128)S(1)}, u32[]{:S(2)}, u32[]{:S(2)}) collective-permute-start(f32[128,1088]{0,1:T(8,128)} %maximum_add_fusion.3), channel_id=1, source_target_pairs={{0,4},{4,8},{8,12},{12,16},{16,20},{20,24},{24,28},{28,32},{32,36}... | collective-permute-start | bytes 1671176 | tf_op jit(solution)/shard_map/while/body/eval_jaxpr/ppermute | solution.py:34
  482.9 15.7 %collective-permute-start = (f32[128,1088]{0,1:T(8,128)}, f32[128,1088]{0,1:T(8,128)S(1)}, u32[]{:S(2)}, u32[]{:S(2)}) collective-permute-start(f32[128,1088]{0,1:T(8,128)} %maximum_add_fusion.3), channel_id=1, source_target_pairs={{0,4},{4,8},{8,12},{12,16},{16,20},{20,24},{24,28},{28,32},{32,36}... | collective-permute-start | bytes 1671176 | tf_op jit(solution)/shard_map/while/body/eval_jaxpr/ppermute | solution.py:34
  504.7 16.8 %collective-permute-start = (f32[128,1088]{0,1:T(8,128)}, f32[128,1088]{0,1:T(8,128)S(1)}, u32[]{:S(2)}, u32[]{:S(2)}) collective-permute-start(f32[128,1088]{0,1:T(8,128)} %maximum_add_fusion.3), channel_id=1, source_target_pairs={{0,4},{4,8},{8,12},{12,16},{16,20},{20,24},{24,28},{28,32},{32,36}... | collective-permute-start | bytes 1671176 | tf_op jit(solution)/shard_map/while/body/eval_jaxpr/ppermute | solution.py:34
  527.7 18.0 %collective-permute-start = (f32[128,1088]{0,1:T(8,128)}, f32[128,1088]{0,1:T(8,128)S(1)}, u32[]{:S(2)}, u32[]{:S(2)}) collective-permute-start(f32[128,1088]{0,1:T(8,128)} %maximum_add_fusion.3), channel_id=1, source_target_pairs={{0,4},{4,8},{8,12},{12,16},{16,20},{20,24},{24,28},{28,32},{32,36}... | collective-permute-start | bytes 1671176 | tf_op jit(solution)/shard_map/while/body/eval_jaxpr/ppermute | solution.py:34
  551.8 19.1 %collective-permute-start = (f32[128,1088]{0,1:T(8,128)}, f32[128,1088]{0,1:T(8,128)S(1)}, u32[]{:S(2)}, u32[]{:S(2)}) collective-permute-start(f32[128,1088]{0,1:T(8,128)} %maximum_add_fusion.3), channel_id=1, source_target_pairs={{0,4},{4,8},{8,12},{12,16},{16,20},{20,24},{24,28},{28,32},{32,36}... | collective-permute-start | bytes 1671176 | tf_op jit(solution)/shard_map/while/body/eval_jaxpr/ppermute | solution.py:34
  577.1 19.6 %collective-permute-start = (f32[128,1088]{0,1:T(8,128)}, f32[128,1088]{0,1:T(8,128)S(1)}, u32[]{:S(2)}, u32[]{:S(2)}) collective-permute-start(f32[128,1088]{0,1:T(8,128)} %maximum_add_fusion.3), channel_id=1, source_target_pairs={{0,4},{4,8},{8,12},{12,16},{16,20},{20,24},{24,28},{28,32},{32,36}... | collective-permute-start | bytes 1671176 | tf_op jit(solution)/shard_map/while/body/eval_jaxpr/ppermute | solution.py:34
  602.9 18.7 %collective-permute-start = (f32[128,1088]{0,1:T(8,128)}, f32[128,1088]{0,1:T(8,128)S(1)}, u32[]{:S(2)}, u32[]{:S(2)}) collective-permute-start(f32[128,1088]{0,1:T(8,128)} %maximum_add_fusion.3), channel_id=1, source_target_pairs={{0,4},{4,8},{8,12},{12,16},{16,20},{20,24},{24,28},{28,32},{32,36}... | collective-permute-start | bytes 1671176 | tf_op jit(solution)/shard_map/while/body/eval_jaxpr/ppermute | solution.py:34
  627.8 17.9 %collective-permute-start = (f32[128,1088]{0,1:T(8,128)}, f32[128,1088]{0,1:T(8,128)S(1)}, u32[]{:S(2)}, u32[]{:S(2)}) collective-permute-start(f32[128,1088]{0,1:T(8,128)} %maximum_add_fusion.3), channel_id=1, source_target_pairs={{0,4},{4,8},{8,12},{12,16},{16,20},{20,24},{24,28},{28,32},{32,36}... | collective-permute-start | bytes 1671176 | tf_op jit(solution)/shard_map/while/body/eval_jaxpr/ppermute | solution.py:34
  651.8 17.0 %collective-permute-start = (f32[128,1088]{0,1:T(8,128)}, f32[128,1088]{0,1:T(8,128)S(1)}, u32[]{:S(2)}, u32[]{:S(2)}) collective-permute-start(f32[128,1088]{0,1:T(8,128)} %maximum_add_fusion.3), channel_id=1, source_target_pairs={{0,4},{4,8},{8,12},{12,16},{16,20},{20,24},{24,28},{28,32},{32,36}... | collective-permute-start | bytes 1671176 | tf_op jit(solution)/shard_map/while/body/eval_jaxpr/ppermute | solution.py:34
  675.0 16.2 %collective-permute-start = (f32[128,1088]{0,1:T(8,128)}, f32[128,1088]{0,1:T(8,128)S(1)}, u32[]{:S(2)}, u32[]{:S(2)}) collective-permute-start(f32[128,1088]{0,1:T(8,128)} %maximum_add_fusion.3), channel_id=1, source_target_pairs={{0,4},{4,8},{8,12},{12,16},{16,20},{20,24},{24,28},{28,32},{32,36}... | collective-permute-start | bytes 1671176 | tf_op jit(solution)/shard_map/while/body/eval_jaxpr/ppermute | solution.py:34
  697.3 15.3 %collective-permute-start = (f32[128,1088]{0,1:T(8,128)}, f32[128,1088]{0,1:T(8,128)S(1)}, u32[]{:S(2)}, u32[]{:S(2)}) collective-permute-start(f32[128,1088]{0,1:T(8,128)} %maximum_add_fusion.3), channel_id=1, source_target_pairs={{0,4},{4,8},{8,12},{12,16},{16,20},{20,24},{24,28},{28,32},{32,36}... | collective-permute-start | bytes 1671176 | tf_op jit(solution)/shard_map/while/body/eval_jaxpr/ppermute | solution.py:34
  718.7 14.4 %collective-permute-start = (f32[128,1088]{0,1:T(8,128)}, f32[128,1088]{0,1:T(8,128)S(1)}, u32[]{:S(2)}, u32[]{:S(2)}) collective-permute-start(f32[128,1088]{0,1:T(8,128)} %maximum_add_fusion.3), channel_id=1, source_target_pairs={{0,4},{4,8},{8,12},{12,16},{16,20},{20,24},{24,28},{28,32},{32,36}... | collective-permute-start | bytes 1671176 | tf_op jit(solution)/shard_map/while/body/eval_jaxpr/ppermute | solution.py:34
  739.3 14.0 %collective-permute-start = (f32[128,1088]{0,1:T(8,128)}, f32[128,1088]{0,1:T(8,128)S(1)}, u32[]{:S(2)}, u32[]{:S(2)}) collective-permute-start(f32[128,1088]{0,1:T(8,128)} %maximum_add_fusion.3), channel_id=1, source_target_pairs={{0,4},{4,8},{8,12},{12,16},{16,20},{20,24},{24,28},{28,32},{32,36}... | collective-permute-start | bytes 1671176 | tf_op jit(solution)/shard_map/while/body/eval_jaxpr/ppermute | solution.py:34
  759.5 14.0 %collective-permute-start = (f32[128,1088]{0,1:T(8,128)}, f32[128,1088]{0,1:T(8,128)S(1)}, u32[]{:S(2)}, u32[]{:S(2)}) collective-permute-start(f32[128,1088]{0,1:T(8,128)} %maximum_add_fusion.3), channel_id=1, source_target_pairs={{0,4},{4,8},{8,12},{12,16},{16,20},{20,24},{24,28},{28,32},{32,36}... | collective-permute-start | bytes 1671176 | tf_op jit(solution)/shard_map/while/body/eval_jaxpr/ppermute | solution.py:34
  779.6 14.0 %collective-permute-start = (f32[128,1088]{0,1:T(8,128)}, f32[128,1088]{0,1:T(8,128)S(1)}, u32[]{:S(2)}, u32[]{:S(2)}) collective-permute-start(f32[128,1088]{0,1:T(8,128)} %maximum_add_fusion.3), channel_id=1, source_target_pairs={{0,4},{4,8},{8,12},{12,16},{16,20},{20,24},{24,28},{28,32},{32,36}... | collective-permute-start | bytes 1671176 | tf_op jit(solution)/shard_map/while/body/eval_jaxpr/ppermute | solution.py:34
  799.7 14.0 %collective-permute-start = (f32[128,1088]{0,1:T(8,128)}, f32[128,1088]{0,1:T(8,128)S(1)}, u32[]{:S(2)}, u32[]{:S(2)}) collective-permute-start(f32[128,1088]{0,1:T(8,128)} %maximum_add_fusion.3), channel_id=1, source_target_pairs={{0,4},{4,8},{8,12},{12,16},{16,20},{20,24},{24,28},{28,32},{32,36}... | collective-permute-start | bytes 1671176 | tf_op jit(solution)/shard_map/while/body/eval_jaxpr/ppermute | solution.py:34
  819.8 14.0 %collective-permute-start = (f32[128,1088]{0,1:T(8,128)}, f32[128,1088]{0,1:T(8,128)S(1)}, u32[]{:S(2)}, u32[]{:S(2)}) collective-permute-start(f32[128,1088]{0,1:T(8,128)} %maximum_add_fusion.3), channel_id=1, source_target_pairs={{0,4},{4,8},{8,12},{12,16},{16,20},{20,24},{24,28},{28,32},{32,36}... | collective-permute-start | bytes 1671176 | tf_op jit(solution)/shard_map/while/body/eval_jaxpr/ppermute | solution.py:34
  840.0 19.3 %collective-permute-start = (f32[128,1088]{0,1:T(8,128)}, f32[128,1088]{0,1:T(8,128)S(1)}, u32[]{:S(2)}, u32[]{:S(2)}) collective-permute-start(f32[128,1088]{0,1:T(8,128)} %maximum_add_fusion.3), channel_id=1, source_target_pairs={{0,4},{4,8},{8,12},{12,16},{16,20},{20,24},{24,28},{28,32},{32,36}... | collective-permute-start | bytes 1671176 | tf_op jit(solution)/shard_map/while/body/eval_jaxpr/ppermute | solution.py:34
  865.5 14.0 %collective-permute-start = (f32[128,1088]{0,1:T(8,128)}, f32[128,1088]{0,1:T(8,128)S(1)}, u32[]{:S(2)}, u32[]{:S(2)}) collective-permute-start(f32[128,1088]{0,1:T(8,128)} %maximum_add_fusion.3), channel_id=1, source_target_pairs={{0,4},{4,8},{8,12},{12,16},{16,20},{20,24},{24,28},{28,32},{32,36}... | collective-permute-start | bytes 1671176 | tf_op jit(solution)/shard_map/while/body/eval_jaxpr/ppermute | solution.py:34
  885.6 17.6 %collective-permute-start = (f32[128,1088]{0,1:T(8,128)}, f32[128,1088]{0,1:T(8,128)S(1)}, u32[]{:S(2)}, u32[]{:S(2)}) collective-permute-start(f32[128,1088]{0,1:T(8,128)} %maximum_add_fusion.3), channel_id=1, source_target_pairs={{0,4},{4,8},{8,12},{12,16},{16,20},{20,24},{24,28},{28,32},{32,36}... | collective-permute-start | bytes 1671176 | tf_op jit(solution)/shard_map/while/body/eval_jaxpr/ppermute | solution.py:34
  903.2 18.8 %copy-start.5 = (bf16[128,576]{0,1:T(8,128)(2,1)S(1)}, bf16[128,576]{0,1:T(8,128)(2,1)}, u32[]{:S(2)}) copy-start(bf16[128,576]{0,1:T(8,128)(2,1)} %param.11) | copy-start | bytes 442372
  903.3 13.8 %collective-permute-start.1 = (f32[128,1088]{0,1:T(8,128)S(1)}, f32[128,1088]{0,1:T(8,128)S(1)}, u32[]{:S(2)}, u32[]{:S(2)}) collective-permute-start(f32[128,1088]{0,1:T(8,128)S(1)} %maximum_add_fusion.1), channel_id=1, source_target_pairs={{0,4},{4,8},{8,12},{12,16},{16,20},{20,24},{24,28},{28,32},{32,36}... | collective-permute-start | bytes 1671176 | tf_op jit(solution)/shard_map/ppermute | solution.py:34
  931.2 23.4 %all-to-all-start.2 = ((f32[32,1,16384]{2,1,0:T(1,128)}), f32[32,1,16384]{2,1,0:T(1,128)}, u32[]{:S(2)}, u32[]{:S(2)}) async-start(f32[32,1,16384]{2,1,0:T(1,128)} %copy.122), calls=%async_computation.2 | async-start | bytes 4194304 | tf_op jit(solution)/shard_map/all_to_all | solution.py:48
  955.7 21.8 %all-to-all-start.1 = ((f32[4,128,576]{1,2,0:T(8,128)}), f32[4,128,576]{1,2,0:T(8,128)S(1)}, u32[]{:S(2)}, u32[]{:S(2)}) async-start(f32[4,128,576]{1,2,0:T(8,128)} %broadcast_in_dim.136), calls=%async_computation.1 | async-start | bytes 2359296 | tf_op jit(solution)/shard_map/all_to_all | solution.py:22
  960.1 25.9 %copy-start.4 = (bf16[128,512]{0,1:T(8,128)(2,1)S(1)}, bf16[128,512]{0,1:T(8,128)(2,1)}, u32[]{:S(2)}) copy-start(bf16[128,512]{0,1:T(8,128)(2,1)} %copy-done.3) | copy-start | bytes 393220
  977.5 3.3 copy-start.2
  980.7 32.4 %all-to-all-start.3 = ((f32[32,1,16384]{2,1,0:T(1,128)}), f32[32,1,16384]{2,1,0:T(1,128)S(1)}, u32[]{:S(2)}, u32[]{:S(2)}) async-start(f32[32,1,16384]{2,1,0:T(1,128)} %broadcast_in_dim.137), calls=%async_computation.3 | async-start | bytes 4194304 | tf_op jit(solution)/shard_map/all_to_all | solution.py:22
Sparse Core Ops, SparseCore 0:
  9.5 142.7 all-gather.1
where the time goes:
time: 1040 us; the launch traced here: 1030 us
  waiting for transfers between devices  647 us (62%)
  matrix products  218 us (21%)
  local copies, waits for them, and re-layouts  63.9 us (6%)
  other arithmetic  61.2 us (6%)
  starting transfers between devices  23.4 us (2%)
  between operations  14.4 us (1%)
    ppermute x32, waiting for transfers between devices, shifted(): return lax.ppermute(value, axis, pairs)  463 us
    all_gather x1, waiting for transfers between devices, shards(): gathered = lax.all_gather(latents, 'seq', axis=0, tiled=True)  123 us
    dot_general x40, matrix products, up_project(): jnp.dot(compressed, value_up, preferred_element_type=jnp.float32)  50.9 us
    dot_general x40, matrix products, up_project(): jnp.dot(compressed, key_up, preferred_element_type=jnp.float32)  50.7 us
    all_to_all x3, waiting for transfers between devices, from_everyone(): lax.all_to_all(jnp.broadcast_to(shard[None], (size, *shard.shape)), axis,...  42.5 us
    dot_general x40, matrix products, scores_of(): jnp.einsum('bhd,kd->hbk', q_rope, rope_keys, preferred_element_type=jnp.f...  39.2 us
    add x63, other arithmetic, grad_block(): return (grads + part, q_acc + q_grad)  29.4 us
    dot_general x32, matrix products, backward_terms(): jnp.einsum('hbk,kd->bhd', dscore, rope_keys, preferred_element_type=jnp.f...  27.9 us
  transfers between devices with their start and end apart: 37, of which 37 were waited for; matrix products, arithmetic and copies ran while one was open for 5% of the time, Pallas kernels for 0%

commit v1 on v0

--- a/solution.py
+++ b/solution.py
@@ -165,7 +165,9 @@
         )
         return (grads + part, q_acc + q_grad)
 
-    gathered = lax.all_gather(latents, "seq", axis=0, tiled=True)
+    gathered = jnp.concatenate(
+        lax.all_to_all(jnp.stack([latents] * lax.axis_size("seq")), "seq", 0, 0), axis=0
+    )
     count = gathered.shape[0]
     width = math.gcd(count, 512)
 

time: 1040 us -> 939 us (0.903)
  waiting for transfers between devices: 647 us -> 566 us
  other arithmetic: 61.2 us -> 28.5 us
  blocking collectives: 0 us -> 17.5 us
  between operations: 14.4 us -> 1.03 us
    all_gather x1 -> x0, waiting for transfers between devices: 123 us -> none  [shards(): gathered = lax.all_gather(latents, 'seq', axis=0, tiled=True)]
    all_to_all x0 -> x1, waiting for transfers between devices: none -> 55.6 us  [shards(): lax.all_to_all(jnp.stack([latents] * lax.axis_size('seq')), 'seq', 0, 0)]
    add x63, other arithmetic: 29.4 us -> 5.5 us  [grad_block(): return (grads + part, q_acc + q_grad)]
    all_to_all x0 -> x1, blocking collectives: none -> 17.5 us  [from_everyone(): lax.all_to_all(jnp.broadcast_to(shard[None], (size, *shard.shape)), axis,...]
    all_to_all x3 -> x2, waiting for transfers between devices: 42.5 us -> 39.8 us  [from_everyone(): lax.all_to_all(jnp.broadcast_to(shard[None], (size, *shard.shape)), axis,...]
  transfers between devices with their start and end apart: 37 -> 36, of which waited for: 37 -> 36; matrix products, arithmetic and copies ran while one was open for 5% -> 5% of each run, Pallas kernels for 0% -> 0%
where the time goes in v1:
time: 939 us; the launch traced here: 930 us
  waiting for transfers between devices  566 us (60%)
  matrix products  226 us (24%)
  local copies, waits for them, and re-layouts  66.6 us (7%)
  other arithmetic  28.5 us (3%)
  starting transfers between devices  20.2 us (2%)
  blocking collectives  17.5 us (2%)
    ppermute x32, waiting for transfers between devices, shifted(): return lax.ppermute(value, axis, pairs)  455 us
    all_to_all x1, waiting for transfers between devices, shards(): lax.all_to_all(jnp.stack([latents] * lax.axis_size('seq')), 'seq', 0, 0)  55.6 us
    dot_general x40, matrix products, up_project(): jnp.dot(compressed, value_up, preferred_element_type=jnp.float32)  49.8 us
    dot_general x40, matrix products, up_project(): jnp.dot(compressed, key_up, preferred_element_type=jnp.float32)  49.7 us
    all_to_all x2, waiting for transfers between devices, from_everyone(): lax.all_to_all(jnp.broadcast_to(shard[None], (size, *shard.shape)), axis,...  39.8 us
    dot_general x40, matrix products, scores_of(): jnp.einsum('bhd,kd->hbk', q_rope, rope_keys, preferred_element_type=jnp.f...  39.2 us
    dot_general x32, matrix products, backward_terms(): jnp.einsum('hbk,kd->bhd', dscore, rope_keys, preferred_element_type=jnp.f...  27.9 us
    dynamic_slice x32, local copies, waits for them, and re-layouts, owner_pos(): return lax.dynamic_slice_in_dim(every_pos, owner_start(step), rows, 0)  24.2 us
  transfers between devices with their start and end apart: 36, of which 36 were waited for; matrix products, arithmetic and copies ran while one was open for 5% of the time, Pallas kernels for 0%

profile of v1, /device:TPU:0, one launch (start us, length us, event | category | flops | bytes accessed | tf_op | source)
XLA Modules:
  0.0 930.4 jit_solution(15934401266809863371)
XLA Ops:
  1.3 17.5 %all_to_all.31 = s32[32,1,128]{2,1,0:T(1,128)} all-to-all(s32[32,1,128]{2,1,0:T(1,128)S(1)} %broadcast_in_dim.132), channel_id=1, replica_groups=mesh['seq'=32,'head'=4] {'seq'}, dimensions={0} | all-to-all | bytes 32768 | tf_op jit(solution)/shard_map/all_to_all | solution.py:22
  18.8 4.2 stack.2
  23.0 5.0 all-to-all-start.1
  29.8 55.6 %all-to-all-done.1 = bf16[32,128,576]{1,2,0:T(8,128)(2,1)} async-done(((bf16[32,128,576]{1,2,0:T(8,128)(2,1)}), bf16[32,128,576]{1,2,0:T(8,128)(2,1)}, u32[]{:S(2)}, u32[]{:S(2)}) %all-to-all-start.1) | async-done | bytes 4718624 | tf_op jit(solution)/shard_map/all_to_all | solution.py:169
  85.4 3.0 copy_bitcast_fusion
  88.4 2.1 copy-done.2
  91.6 1.8 fusion.47
  93.4 66.3 %while.36 = (s32[]{:T(128)}, f32[4,128]{1,0:T(4,128)S(1)}, f32[4,128]{1,0:T(4,128)S(1)}, f32[4,128]{1,0:T(4,128)}, s32[4096]{0:T(1024)}, /*index=5*/s32[128]{0:T...) while((s32[]{:T(128)}, f32[4,128]{1,0:T(4,128)S(1)}, ...), condition=%wide.region_4.5_spmd.clone, body=%wide.region_0.4_spmd.clone.sunk | while | flops 708120064 | bytes 10136302 | solution.py:178
  93.4 1.5 convolution_convert_fusion.9
  97.6 1.5 convolution_convert_fusion.10
  105.3 1.5 convolution_convert_fusion.10
  109.4 1.5 convolution_convert_fusion.9
  113.6 1.5 convolution_convert_fusion.10
  117.8 1.5 convolution_convert_fusion.9
  122.0 1.5 convolution_convert_fusion.10
  130.4 1.5 convolution_convert_fusion.10
  134.5 1.5 convolution_convert_fusion.9
  138.7 1.5 convolution_convert_fusion.10
  147.1 1.5 convolution_convert_fusion.10
  155.5 1.5 convolution_convert_fusion.10
  165.6 647.2 %while.37 = (s32[]{:T(128)}, f32[128,1088]{0,1:T(8,128)S(1)}, f32[128,768]{0,1:T(8,128)}, s32[]{:T(128)}, s32[4096]{0:T(1024)}, /*index=5*/s32[128]{0:T(128)S(1)...) while((s32[]{:T(128)}, f32[128,1088]{0,1:T(8,128)S(1)}, ...), condition=%wide.region_6.7_spmd.clone, body=%wide.region_5.6_spmd.clone.sunk | while | flops 244719632 | bytes 14883310 | solution.py:189
  172.3 14.7 %collective-permute-done = f32[128,1088]{0,1:T(8,128)S(1)} collective-permute-done((f32[128,1088]{0,1:T(8,128)S(1)}, f32[128,1088]{0,1:T(8,128)S(1)}, u32[]{:S(2)}, u32[]{:S(2)}) %collective-permute-start) | collective-permute-done | bytes 557088 | tf_op jit(solution)/shard_map/while/body/eval_jaxpr/ppermute | solution.py:34
  193.7 13.8 %collective-permute-done = f32[128,1088]{0,1:T(8,128)S(1)} collective-permute-done((f32[128,1088]{0,1:T(8,128)S(1)}, f32[128,1088]{0,1:T(8,128)S(1)}, u32[]{:S(2)}, u32[]{:S(2)}) %collective-permute-start) | collective-permute-done | bytes 557088 | tf_op jit(solution)/shard_map/while/body/eval_jaxpr/ppermute | solution.py:34
  214.2 13.0 %collective-permute-done = f32[128,1088]{0,1:T(8,128)S(1)} collective-permute-done((f32[128,1088]{0,1:T(8,128)S(1)}, f32[128,1088]{0,1:T(8,128)S(1)}, u32[]{:S(2)}, u32[]{:S(2)}) %collective-permute-start) | collective-permute-done | bytes 557088 | tf_op jit(solution)/shard_map/while/body/eval_jaxpr/ppermute | solution.py:34
  233.8 12.5 %collective-permute-done = f32[128,1088]{0,1:T(8,128)S(1)} collective-permute-done((f32[128,1088]{0,1:T(8,128)S(1)}, f32[128,1088]{0,1:T(8,128)S(1)}, u32[]{:S(2)}, u32[]{:S(2)}) %collective-permute-start) | collective-permute-done | bytes 557088 | tf_op jit(solution)/shard_map/while/body/eval_jaxpr/ppermute | solution.py:34
  253.1 12.5 %collective-permute-done = f32[128,1088]{0,1:T(8,128)S(1)} collective-permute-done((f32[128,1088]{0,1:T(8,128)S(1)}, f32[128,1088]{0,1:T(8,128)S(1)}, u32[]{:S(2)}, u32[]{:S(2)}) %collective-permute-start) | collective-permute-done | bytes 557088 | tf_op jit(solution)/shard_map/while/body/eval_jaxpr/ppermute | solution.py:34
  272.3 12.5 %collective-permute-done = f32[128,1088]{0,1:T(8,128)S(1)} collective-permute-done((f32[128,1088]{0,1:T(8,128)S(1)}, f32[128,1088]{0,1:T(8,128)S(1)}, u32[]{:S(2)}, u32[]{:S(2)}) %collective-permute-start) | collective-permute-done | bytes 557088 | tf_op jit(solution)/shard_map/while/body/eval_jaxpr/ppermute | solution.py:34
  291.5 12.5 %collective-permute-done = f32[128,1088]{0,1:T(8,128)S(1)} collective-permute-done((f32[128,1088]{0,1:T(8,128)S(1)}, f32[128,1088]{0,1:T(8,128)S(1)}, u32[]{:S(2)}, u32[]{:S(2)}) %collective-permute-start) | collective-permute-done | bytes 557088 | tf_op jit(solution)/shard_map/while/body/eval_jaxpr/ppermute | solution.py:34
  310.7 12.5 %collective-permute-done = f32[128,1088]{0,1:T(8,128)S(1)} collective-permute-done((f32[128,1088]{0,1:T(8,128)S(1)}, f32[128,1088]{0,1:T(8,128)S(1)}, u32[]{:S(2)}, u32[]{:S(2)}) %collective-permute-start) | collective-permute-done | bytes 557088 | tf_op jit(solution)/shard_map/while/body/eval_jaxpr/ppermute | solution.py:34
  330.0 12.6 %collective-permute-done = f32[128,1088]{0,1:T(8,128)S(1)} collective-permute-done((f32[128,1088]{0,1:T(8,128)S(1)}, f32[128,1088]{0,1:T(8,128)S(1)}, u32[]{:S(2)}, u32[]{:S(2)}) %collective-permute-start) | collective-permute-done | bytes 557088 | tf_op jit(solution)/shard_map/while/body/eval_jaxpr/ppermute | solution.py:34
  349.2 13.7 %collective-permute-done = f32[128,1088]{0,1:T(8,128)S(1)} collective-permute-done((f32[128,1088]{0,1:T(8,128)S(1)}, f32[128,1088]{0,1:T(8,128)S(1)}, u32[]{:S(2)}, u32[]{:S(2)}) %collective-permute-start) | collective-permute-done | bytes 557088 | tf_op jit(solution)/shard_map/while/body/eval_jaxpr/ppermute | solution.py:34
  369.7 14.9 %collective-permute-done = f32[128,1088]{0,1:T(8,128)S(1)} collective-permute-done((f32[128,1088]{0,1:T(8,128)S(1)}, f32[128,1088]{0,1:T(8,128)S(1)}, u32[]{:S(2)}, u32[]{:S(2)}) %collective-permute-start) | collective-permute-done | bytes 557088 | tf_op jit(solution)/shard_map/while/body/eval_jaxpr/ppermute | solution.py:34
  391.2 16.0 %collective-permute-done = f32[128,1088]{0,1:T(8,128)S(1)} collective-permute-done((f32[128,1088]{0,1:T(8,128)S(1)}, f32[128,1088]{0,1:T(8,128)S(1)}, u32[]{:S(2)}, u32[]{:S(2)}) %collective-permute-start) | collective-permute-done | bytes 557088 | tf_op jit(solution)/shard_map/while/body/eval_jaxpr/ppermute | solution.py:34
  413.9 17.2 %collective-permute-done = f32[128,1088]{0,1:T(8,128)S(1)} collective-permute-done((f32[128,1088]{0,1:T(8,128)S(1)}, f32[128,1088]{0,1:T(8,128)S(1)}, u32[]{:S(2)}, u32[]{:S(2)}) %collective-permute-start) | collective-permute-done | bytes 557088 | tf_op jit(solution)/shard_map/while/body/eval_jaxpr/ppermute | solution.py:34
  437.8 18.3 %collective-permute-done = f32[128,1088]{0,1:T(8,128)S(1)} collective-permute-done((f32[128,1088]{0,1:T(8,128)S(1)}, f32[128,1088]{0,1:T(8,128)S(1)}, u32[]{:S(2)}, u32[]{:S(2)}) %collective-permute-start) | collective-permute-done | bytes 557088 | tf_op jit(solution)/shard_map/while/body/eval_jaxpr/ppermute | solution.py:34
  462.8 17.6 %collective-permute-done = f32[128,1088]{0,1:T(8,128)S(1)} collective-permute-done((f32[128,1088]{0,1:T(8,128)S(1)}, f32[128,1088]{0,1:T(8,128)S(1)}, u32[]{:S(2)}, u32[]{:S(2)}) %collective-permute-start) | collective-permute-done | bytes 557088 | tf_op jit(solution)/shard_map/while/body/eval_jaxpr/ppermute | solution.py:34
  487.1 16.8 %collective-permute-done = f32[128,1088]{0,1:T(8,128)S(1)} collective-permute-done((f32[128,1088]{0,1:T(8,128)S(1)}, f32[128,1088]{0,1:T(8,128)S(1)}, u32[]{:S(2)}, u32[]{:S(2)}) %collective-permute-start) | collective-permute-done | bytes 557088 | tf_op jit(solution)/shard_map/while/body/eval_jaxpr/ppermute | solution.py:34
  510.6 15.9 %collective-permute-done = f32[128,1088]{0,1:T(8,128)S(1)} collective-permute-done((f32[128,1088]{0,1:T(8,128)S(1)}, f32[128,1088]{0,1:T(8,128)S(1)}, u32[]{:S(2)}, u32[]{:S(2)}) %collective-permute-start) | collective-permute-done | bytes 557088 | tf_op jit(solution)/shard_map/while/body/eval_jaxpr/ppermute | solution.py:34
  533.2 15.1 %collective-permute-done = f32[128,1088]{0,1:T(8,128)S(1)} collective-permute-done((f32[128,1088]{0,1:T(8,128)S(1)}, f32[128,1088]{0,1:T(8,128)S(1)}, u32[]{:S(2)}, u32[]{:S(2)}) %collective-permute-start) | collective-permute-done | bytes 557088 | tf_op jit(solution)/shard_map/while/body/eval_jaxpr/ppermute | solution.py:34
  555.0 14.2 %collective-permute-done = f32[128,1088]{0,1:T(8,128)S(1)} collective-permute-done((f32[128,1088]{0,1:T(8,128)S(1)}, f32[128,1088]{0,1:T(8,128)S(1)}, u32[]{:S(2)}, u32[]{:S(2)}) %collective-permute-start) | collective-permute-done | bytes 557088 | tf_op jit(solution)/shard_map/while/body/eval_jaxpr/ppermute | solution.py:34
  575.9 13.4 %collective-permute-done = f32[128,1088]{0,1:T(8,128)S(1)} collective-permute-done((f32[128,1088]{0,1:T(8,128)S(1)}, f32[128,1088]{0,1:T(8,128)S(1)}, u32[]{:S(2)}, u32[]{:S(2)}) %collective-permute-start) | collective-permute-done | bytes 557088 | tf_op jit(solution)/shard_map/while/body/eval_jaxpr/ppermute | solution.py:34
  596.0 12.5 %collective-permute-done = f32[128,1088]{0,1:T(8,128)S(1)} collective-permute-done((f32[128,1088]{0,1:T(8,128)S(1)}, f32[128,1088]{0,1:T(8,128)S(1)}, u32[]{:S(2)}, u32[]{:S(2)}) %collective-permute-start) | collective-permute-done | bytes 557088 | tf_op jit(solution)/shard_map/while/body/eval_jaxpr/ppermute | solution.py:34
  615.2 12.5 %collective-permute-done = f32[128,1088]{0,1:T(8,128)S(1)} collective-permute-done((f32[128,1088]{0,1:T(8,128)S(1)}, f32[128,1088]{0,1:T(8,128)S(1)}, u32[]{:S(2)}, u32[]{:S(2)}) %collective-permute-start) | collective-permute-done | bytes 557088 | tf_op jit(solution)/shard_map/while/body/eval_jaxpr/ppermute | solution.py:34
  634.5 12.5 %collective-permute-done = f32[128,1088]{0,1:T(8,128)S(1)} collective-permute-done((f32[128,1088]{0,1:T(8,128)S(1)}, f32[128,1088]{0,1:T(8,128)S(1)}, u32[]{:S(2)}, u32[]{:S(2)}) %collective-permute-start) | collective-permute-done | bytes 557088 | tf_op jit(solution)/shard_map/while/body/eval_jaxpr/ppermute | solution.py:34
  653.7 12.5 %collective-permute-done = f32[128,1088]{0,1:T(8,128)S(1)} collective-permute-done((f32[128,1088]{0,1:T(8,128)S(1)}, f32[128,1088]{0,1:T(8,128)S(1)}, u32[]{:S(2)}, u32[]{:S(2)}) %collective-permute-start) | collective-permute-done | bytes 557088 | tf_op jit(solution)/shard_map/while/body/eval_jaxpr/ppermute | solution.py:34
  672.9 12.5 %collective-permute-done = f32[128,1088]{0,1:T(8,128)S(1)} collective-permute-done((f32[128,1088]{0,1:T(8,128)S(1)}, f32[128,1088]{0,1:T(8,128)S(1)}, u32[]{:S(2)}, u32[]{:S(2)}) %collective-permute-start) | collective-permute-done | bytes 557088 | tf_op jit(solution)/shard_map/while/body/eval_jaxpr/ppermute | solution.py:34
  692.2 12.5 %collective-permute-done = f32[128,1088]{0,1:T(8,128)S(1)} collective-permute-done((f32[128,1088]{0,1:T(8,128)S(1)}, f32[128,1088]{0,1:T(8,128)S(1)}, u32[]{:S(2)}, u32[]{:S(2)}) %collective-permute-start) | collective-permute-done | bytes 557088 | tf_op jit(solution)/shard_map/while/body/eval_jaxpr/ppermute | solution.py:34
  711.4 13.3 %collective-permute-done = f32[128,1088]{0,1:T(8,128)S(1)} collective-permute-done((f32[128,1088]{0,1:T(8,128)S(1)}, f32[128,1088]{0,1:T(8,128)S(1)}, u32[]{:S(2)}, u32[]{:S(2)}) %collective-permute-start) | collective-permute-done | bytes 557088 | tf_op jit(solution)/shard_map/while/body/eval_jaxpr/ppermute | solution.py:34
  731.4 14.5 %collective-permute-done = f32[128,1088]{0,1:T(8,128)S(1)} collective-permute-done((f32[128,1088]{0,1:T(8,128)S(1)}, f32[128,1088]{0,1:T(8,128)S(1)}, u32[]{:S(2)}, u32[]{:S(2)}) %collective-permute-start) | collective-permute-done | bytes 557088 | tf_op jit(solution)/shard_map/while/body/eval_jaxpr/ppermute | solution.py:34
  752.6 15.6 %collective-permute-done = f32[128,1088]{0,1:T(8,128)S(1)} collective-permute-done((f32[128,1088]{0,1:T(8,128)S(1)}, f32[128,1088]{0,1:T(8,128)S(1)}, u32[]{:S(2)}, u32[]{:S(2)}) %collective-permute-start) | collective-permute-done | bytes 557088 | tf_op jit(solution)/shard_map/while/body/eval_jaxpr/ppermute | solution.py:34
  774.9 16.0 %collective-permute-done = f32[128,1088]{0,1:T(8,128)S(1)} collective-permute-done((f32[128,1088]{0,1:T(8,128)S(1)}, f32[128,1088]{0,1:T(8,128)S(1)}, u32[]{:S(2)}, u32[]{:S(2)}) %collective-permute-start) | collective-permute-done | bytes 557088 | tf_op jit(solution)/shard_map/while/body/eval_jaxpr/ppermute | solution.py:34
  797.5 15.2 %collective-permute-done = f32[128,1088]{0,1:T(8,128)S(1)} collective-permute-done((f32[128,1088]{0,1:T(8,128)S(1)}, f32[128,1088]{0,1:T(8,128)S(1)}, u32[]{:S(2)}, u32[]{:S(2)}) %collective-permute-start) | collective-permute-done | bytes 557088 | tf_op jit(solution)/shard_map/while/body/eval_jaxpr/ppermute | solution.py:34
  813.9 15.1 %collective-permute-done.1 = f32[128,1088]{0,1:T(8,128)S(1)} collective-permute-done((f32[128,1088]{0,1:T(8,128)S(1)}, f32[128,1088]{0,1:T(8,128)S(1)}, u32[]{:S(2)}, u32[]{:S(2)}) %collective-permute-start.1) | collective-permute-done | bytes 557088 | tf_op jit(solution)/shard_map/ppermute | solution.py:34
  835.8 3.5 copy.123
  839.3 4.2 all-to-all-start.3
  846.3 15.6 %all-to-all-done.3 = f32[32,1,16384]{2,1,0:T(1,128)S(1)} async-done(((f32[32,1,16384]{2,1,0:T(1,128)}), f32[32,1,16384]{2,1,0:T(1,128)S(1)}, u32[]{:S(2)}, u32[]{:S(2)}) %all-to-all-start.3) | async-done | bytes 2097184 | tf_op jit(solution)/shard_map/all_to_all | solution.py:48
  863.1 4.3 all-to-all-start.2
  868.8 16.0 %all-to-all-done.2 = f32[4,128,576]{1,2,0:T(8,128)} async-done(((f32[4,128,576]{1,2,0:T(8,128)}), f32[4,128,576]{1,2,0:T(8,128)}, u32[]{:S(2)}, u32[]{:S(2)}) %all-to-all-start.2) | async-done | bytes 1179680 | tf_op jit(solution)/shard_map/all_to_all | solution.py:22
  884.8 3.3 broadcast_in_dim.137
  888.0 4.3 all-to-all-start.4
  894.5 2.1 reduce_sum.44
  896.6 23.8 %all-to-all-done.4 = f32[32,1,16384]{2,1,0:T(1,128)S(1)} async-done(((f32[32,1,16384]{2,1,0:T(1,128)}), f32[32,1,16384]{2,1,0:T(1,128)S(1)}, u32[]{:S(2)}, u32[]{:S(2)}) %all-to-all-start.4) | async-done | bytes 2097184 | tf_op jit(solution)/shard_map/all_to_all | solution.py:22
  920.4 6.5 slice_reduce_fusion
  926.9 2.4 reshape.268
  (794 shorter events, 276.7 us)
Async XLA Ops:
  23.0 62.4 %all-to-all-start.1 = ((bf16[32,128,576]{1,2,0:T(8,128)(2,1)}), bf16[32,128,576]{1,2,0:T(8,128)(2,1)}, u32[]{:S(2)}, u32[]{:S(2)}) async-start(bf16[32,128,576]{1,2,0:T(8,128)(2,1)} %stack.2), calls=%async_computation.1 | async-start | bytes 9437184 | tf_op jit(solution)/shard_map/all_to_all | solution.py:169
  29.8 60.7 %copy-start.1 = (bf16[512,512]{1,0:T(8,128)(2,1)S(1)}, bf16[512,512]{1,0:T(8,128)(2,1)}, u32[]{:S(2)}) copy-start(bf16[512,512]{1,0:T(8,128)(2,1)} %param.12) | copy-start | bytes 1572868
  29.8 61.8 %copy-start = (bf16[512,512]{1,0:T(8,128)(2,1)S(1)}, bf16[512,512]{1,0:T(8,128)(2,1)}, u32[]{:S(2)}) copy-start(bf16[512,512]{1,0:T(8,128)(2,1)} %param.13) | copy-start | bytes 1572868
  171.0 16.0 %collective-permute-start = (f32[128,1088]{0,1:T(8,128)S(1)}, f32[128,1088]{0,1:T(8,128)S(1)}, u32[]{:S(2)}, u32[]{:S(2)}) collective-permute-start(f32[128,1088]{0,1:T(8,128)S(1)} %maximum_add_fusion.3), channel_id=1, source_target_pairs={{0,4},{4,8},{8,12},{12,16},{16,20},{20,24},{24,28},{28,32},{32,36}... | collective-permute-start | bytes 1671176 | tf_op jit(solution)/shard_map/while/body/eval_jaxpr/ppermute | solution.py:34
  172.3 14.7 %copy-start.4 = (f32[128,768]{0,1:T(8,128)}, f32[128,768]{0,1:T(8,128)S(1)}, u32[]{:S(2)}) copy-start(f32[128,768]{0,1:T(8,128)S(1)} %bitcast_add_fusion.2) | copy-start | bytes 1179652 | tf_op jit(solution)/shard_map/while
  192.4 15.1 %collective-permute-start = (f32[128,1088]{0,1:T(8,128)S(1)}, f32[128,1088]{0,1:T(8,128)S(1)}, u32[]{:S(2)}, u32[]{:S(2)}) collective-permute-start(f32[128,1088]{0,1:T(8,128)S(1)} %maximum_add_fusion.3), channel_id=1, source_target_pairs={{0,4},{4,8},{8,12},{12,16},{16,20},{20,24},{24,28},{28,32},{32,36}... | collective-permute-start | bytes 1671176 | tf_op jit(solution)/shard_map/while/body/eval_jaxpr/ppermute | solution.py:34
  193.7 13.8 %copy-start.4 = (f32[128,768]{0,1:T(8,128)}, f32[128,768]{0,1:T(8,128)S(1)}, u32[]{:S(2)}) copy-start(f32[128,768]{0,1:T(8,128)S(1)} %bitcast_add_fusion.2) | copy-start | bytes 1179652 | tf_op jit(solution)/shard_map/while
  212.9 14.2 %collective-permute-start = (f32[128,1088]{0,1:T(8,128)S(1)}, f32[128,1088]{0,1:T(8,128)S(1)}, u32[]{:S(2)}, u32[]{:S(2)}) collective-permute-start(f32[128,1088]{0,1:T(8,128)S(1)} %maximum_add_fusion.3), channel_id=1, source_target_pairs={{0,4},{4,8},{8,12},{12,16},{16,20},{20,24},{24,28},{28,32},{32,36}... | collective-permute-start | bytes 1671176 | tf_op jit(solution)/shard_map/while/body/eval_jaxpr/ppermute | solution.py:34
  214.2 13.0 %copy-start.4 = (f32[128,768]{0,1:T(8,128)}, f32[128,768]{0,1:T(8,128)S(1)}, u32[]{:S(2)}) copy-start(f32[128,768]{0,1:T(8,128)S(1)} %bitcast_add_fusion.2) | copy-start | bytes 1179652 | tf_op jit(solution)/shard_map/while
  232.5 13.8 %collective-permute-start = (f32[128,1088]{0,1:T(8,128)S(1)}, f32[128,1088]{0,1:T(8,128)S(1)}, u32[]{:S(2)}, u32[]{:S(2)}) collective-permute-start(f32[128,1088]{0,1:T(8,128)S(1)} %maximum_add_fusion.3), channel_id=1, source_target_pairs={{0,4},{4,8},{8,12},{12,16},{16,20},{20,24},{24,28},{28,32},{32,36}... | collective-permute-start | bytes 1671176 | tf_op jit(solution)/shard_map/while/body/eval_jaxpr/ppermute | solution.py:34
  233.8 12.5 %copy-start.4 = (f32[128,768]{0,1:T(8,128)}, f32[128,768]{0,1:T(8,128)S(1)}, u32[]{:S(2)}) copy-start(f32[128,768]{0,1:T(8,128)S(1)} %bitcast_add_fusion.2) | copy-start | bytes 1179652 | tf_op jit(solution)/shard_map/while
  251.8 13.8 %collective-permute-start = (f32[128,1088]{0,1:T(8,128)S(1)}, f32[128,1088]{0,1:T(8,128)S(1)}, u32[]{:S(2)}, u32[]{:S(2)}) collective-permute-start(f32[128,1088]{0,1:T(8,128)S(1)} %maximum_add_fusion.3), channel_id=1, source_target_pairs={{0,4},{4,8},{8,12},{12,16},{16,20},{20,24},{24,28},{28,32},{32,36}... | collective-permute-start | bytes 1671176 | tf_op jit(solution)/shard_map/while/body/eval_jaxpr/ppermute | solution.py:34
  253.0 12.5 %copy-start.4 = (f32[128,768]{0,1:T(8,128)}, f32[128,768]{0,1:T(8,128)S(1)}, u32[]{:S(2)}) copy-start(f32[128,768]{0,1:T(8,128)S(1)} %bitcast_add_fusion.2) | copy-start | bytes 1179652 | tf_op jit(solution)/shard_map/while
  271.0 13.8 %collective-permute-start = (f32[128,1088]{0,1:T(8,128)S(1)}, f32[128,1088]{0,1:T(8,128)S(1)}, u32[]{:S(2)}, u32[]{:S(2)}) collective-permute-start(f32[128,1088]{0,1:T(8,128)S(1)} %maximum_add_fusion.3), channel_id=1, source_target_pairs={{0,4},{4,8},{8,12},{12,16},{16,20},{20,24},{24,28},{28,32},{32,36}... | collective-permute-start | bytes 1671176 | tf_op jit(solution)/shard_map/while/body/eval_jaxpr/ppermute | solution.py:34
  290.2 13.8 %collective-permute-start = (f32[128,1088]{0,1:T(8,128)S(1)}, f32[128,1088]{0,1:T(8,128)S(1)}, u32[]{:S(2)}, u32[]{:S(2)}) collective-permute-start(f32[128,1088]{0,1:T(8,128)S(1)} %maximum_add_fusion.3), channel_id=1, source_target_pairs={{0,4},{4,8},{8,12},{12,16},{16,20},{20,24},{24,28},{28,32},{32,36}... | collective-permute-start | bytes 1671176 | tf_op jit(solution)/shard_map/while/body/eval_jaxpr/ppermute | solution.py:34
  309.5 13.8 %collective-permute-start = (f32[128,1088]{0,1:T(8,128)S(1)}, f32[128,1088]{0,1:T(8,128)S(1)}, u32[]{:S(2)}, u32[]{:S(2)}) collective-permute-start(f32[128,1088]{0,1:T(8,128)S(1)} %maximum_add_fusion.3), channel_id=1, source_target_pairs={{0,4},{4,8},{8,12},{12,16},{16,20},{20,24},{24,28},{28,32},{32,36}... | collective-permute-start | bytes 1671176 | tf_op jit(solution)/shard_map/while/body/eval_jaxpr/ppermute | solution.py:34
  328.7 13.9 %collective-permute-start = (f32[128,1088]{0,1:T(8,128)S(1)}, f32[128,1088]{0,1:T(8,128)S(1)}, u32[]{:S(2)}, u32[]{:S(2)}) collective-permute-start(f32[128,1088]{0,1:T(8,128)S(1)} %maximum_add_fusion.3), channel_id=1, source_target_pairs={{0,4},{4,8},{8,12},{12,16},{16,20},{20,24},{24,28},{28,32},{32,36}... | collective-permute-start | bytes 1671176 | tf_op jit(solution)/shard_map/while/body/eval_jaxpr/ppermute | solution.py:34
  330.0 12.6 %copy-start.4 = (f32[128,768]{0,1:T(8,128)}, f32[128,768]{0,1:T(8,128)S(1)}, u32[]{:S(2)}) copy-start(f32[128,768]{0,1:T(8,128)S(1)} %bitcast_add_fusion.2) | copy-start | bytes 1179652 | tf_op jit(solution)/shard_map/while
  348.0 15.0 %collective-permute-start = (f32[128,1088]{0,1:T(8,128)S(1)}, f32[128,1088]{0,1:T(8,128)S(1)}, u32[]{:S(2)}, u32[]{:S(2)}) collective-permute-start(f32[128,1088]{0,1:T(8,128)S(1)} %maximum_add_fusion.3), channel_id=1, source_target_pairs={{0,4},{4,8},{8,12},{12,16},{16,20},{20,24},{24,28},{28,32},{32,36}... | collective-permute-start | bytes 1671176 | tf_op jit(solution)/shard_map/while/body/eval_jaxpr/ppermute | solution.py:34
  349.2 13.7 %copy-start.4 = (f32[128,768]{0,1:T(8,128)}, f32[128,768]{0,1:T(8,128)S(1)}, u32[]{:S(2)}) copy-start(f32[128,768]{0,1:T(8,128)S(1)} %bitcast_add_fusion.2) | copy-start | bytes 1179652 | tf_op jit(solution)/shard_map/while
  368.4 16.2 %collective-permute-start = (f32[128,1088]{0,1:T(8,128)S(1)}, f32[128,1088]{0,1:T(8,128)S(1)}, u32[]{:S(2)}, u32[]{:S(2)}) collective-permute-start(f32[128,1088]{0,1:T(8,128)S(1)} %maximum_add_fusion.3), channel_id=1, source_target_pairs={{0,4},{4,8},{8,12},{12,16},{16,20},{20,24},{24,28},{28,32},{32,36}... | collective-permute-start | bytes 1671176 | tf_op jit(solution)/shard_map/while/body/eval_jaxpr/ppermute | solution.py:34
  369.6 14.9 %copy-start.4 = (f32[128,768]{0,1:T(8,128)}, f32[128,768]{0,1:T(8,128)S(1)}, u32[]{:S(2)}) copy-start(f32[128,768]{0,1:T(8,128)S(1)} %bitcast_add_fusion.2) | copy-start | bytes 1179652 | tf_op jit(solution)/shard_map/while
  389.9 17.3 %collective-permute-start = (f32[128,1088]{0,1:T(8,128)S(1)}, f32[128,1088]{0,1:T(8,128)S(1)}, u32[]{:S(2)}, u32[]{:S(2)}) collective-permute-start(f32[128,1088]{0,1:T(8,128)S(1)} %maximum_add_fusion.3), channel_id=1, source_target_pairs={{0,4},{4,8},{8,12},{12,16},{16,20},{20,24},{24,28},{28,32},{32,36}... | collective-permute-start | bytes 1671176 | tf_op jit(solution)/shard_map/while/body/eval_jaxpr/ppermute | solution.py:34
  391.2 16.0 %copy-start.4 = (f32[128,768]{0,1:T(8,128)}, f32[128,768]{0,1:T(8,128)S(1)}, u32[]{:S(2)}) copy-start(f32[128,768]{0,1:T(8,128)S(1)} %bitcast_add_fusion.2) | copy-start | bytes 1179652 | tf_op jit(solution)/shard_map/while
  412.6 18.4 %collective-permute-start = (f32[128,1088]{0,1:T(8,128)S(1)}, f32[128,1088]{0,1:T(8,128)S(1)}, u32[]{:S(2)}, u32[]{:S(2)}) collective-permute-start(f32[128,1088]{0,1:T(8,128)S(1)} %maximum_add_fusion.3), channel_id=1, source_target_pairs={{0,4},{4,8},{8,12},{12,16},{16,20},{20,24},{24,28},{28,32},{32,36}... | collective-permute-start | bytes 1671176 | tf_op jit(solution)/shard_map/while/body/eval_jaxpr/ppermute | solution.py:34
  413.9 17.2 %copy-start.4 = (f32[128,768]{0,1:T(8,128)}, f32[128,768]{0,1:T(8,128)S(1)}, u32[]{:S(2)}) copy-start(f32[128,768]{0,1:T(8,128)S(1)} %bitcast_add_fusion.2) | copy-start | bytes 1179652 | tf_op jit(solution)/shard_map/while
  436.5 19.6 %collective-permute-start = (f32[128,1088]{0,1:T(8,128)S(1)}, f32[128,1088]{0,1:T(8,128)S(1)}, u32[]{:S(2)}, u32[]{:S(2)}) collective-permute-start(f32[128,1088]{0,1:T(8,128)S(1)} %maximum_add_fusion.3), channel_id=1, source_target_pairs={{0,4},{4,8},{8,12},{12,16},{16,20},{20,24},{24,28},{28,32},{32,36}... | collective-permute-start | bytes 1671176 | tf_op jit(solution)/shard_map/while/body/eval_jaxpr/ppermute | solution.py:34
  437.8 18.3 %copy-start.4 = (f32[128,768]{0,1:T(8,128)}, f32[128,768]{0,1:T(8,128)S(1)}, u32[]{:S(2)}) copy-start(f32[128,768]{0,1:T(8,128)S(1)} %bitcast_add_fusion.2) | copy-start | bytes 1179652 | tf_op jit(solution)/shard_map/while
  461.5 18.9 %collective-permute-start = (f32[128,1088]{0,1:T(8,128)S(1)}, f32[128,1088]{0,1:T(8,128)S(1)}, u32[]{:S(2)}, u32[]{:S(2)}) collective-permute-start(f32[128,1088]{0,1:T(8,128)S(1)} %maximum_add_fusion.3), channel_id=1, source_target_pairs={{0,4},{4,8},{8,12},{12,16},{16,20},{20,24},{24,28},{28,32},{32,36}... | collective-permute-start | bytes 1671176 | tf_op jit(solution)/shard_map/while/body/eval_jaxpr/ppermute | solution.py:34
  462.7 17.7 %copy-start.4 = (f32[128,768]{0,1:T(8,128)}, f32[128,768]{0,1:T(8,128)S(1)}, u32[]{:S(2)}) copy-start(f32[128,768]{0,1:T(8,128)S(1)} %bitcast_add_fusion.2) | copy-start | bytes 1179652 | tf_op jit(solution)/shard_map/while
  485.8 18.1 %collective-permute-start = (f32[128,1088]{0,1:T(8,128)S(1)}, f32[128,1088]{0,1:T(8,128)S(1)}, u32[]{:S(2)}, u32[]{:S(2)}) collective-permute-start(f32[128,1088]{0,1:T(8,128)S(1)} %maximum_add_fusion.3), channel_id=1, source_target_pairs={{0,4},{4,8},{8,12},{12,16},{16,20},{20,24},{24,28},{28,32},{32,36}... | collective-permute-start | bytes 1671176 | tf_op jit(solution)/shard_map/while/body/eval_jaxpr/ppermute | solution.py:34
  487.1 16.8 %copy-start.4 = (f32[128,768]{0,1:T(8,128)}, f32[128,768]{0,1:T(8,128)S(1)}, u32[]{:S(2)}) copy-start(f32[128,768]{0,1:T(8,128)S(1)} %bitcast_add_fusion.2) | copy-start | bytes 1179652 | tf_op jit(solution)/shard_map/while
  509.3 17.2 %collective-permute-start = (f32[128,1088]{0,1:T(8,128)S(1)}, f32[128,1088]{0,1:T(8,128)S(1)}, u32[]{:S(2)}, u32[]{:S(2)}) collective-permute-start(f32[128,1088]{0,1:T(8,128)S(1)} %maximum_add_fusion.3), channel_id=1, source_target_pairs={{0,4},{4,8},{8,12},{12,16},{16,20},{20,24},{24,28},{28,32},{32,36}... | collective-permute-start | bytes 1671176 | tf_op jit(solution)/shard_map/while/body/eval_jaxpr/ppermute | solution.py:34
  510.6 16.0 %copy-start.4 = (f32[128,768]{0,1:T(8,128)}, f32[128,768]{0,1:T(8,128)S(1)}, u32[]{:S(2)}) copy-start(f32[128,768]{0,1:T(8,128)S(1)} %bitcast_add_fusion.2) | copy-start | bytes 1179652 | tf_op jit(solution)/shard_map/while
  531.9 16.4 %collective-permute-start = (f32[128,1088]{0,1:T(8,128)S(1)}, f32[128,1088]{0,1:T(8,128)S(1)}, u32[]{:S(2)}, u32[]{:S(2)}) collective-permute-start(f32[128,1088]{0,1:T(8,128)S(1)} %maximum_add_fusion.3), channel_id=1, source_target_pairs={{0,4},{4,8},{8,12},{12,16},{16,20},{20,24},{24,28},{28,32},{32,36}... | collective-permute-start | bytes 1671176 | tf_op jit(solution)/shard_map/while/body/eval_jaxpr/ppermute | solution.py:34
  533.2 15.1 %copy-start.4 = (f32[128,768]{0,1:T(8,128)}, f32[128,768]{0,1:T(8,128)S(1)}, u32[]{:S(2)}) copy-start(f32[128,768]{0,1:T(8,128)S(1)} %bitcast_add_fusion.2) | copy-start | bytes 1179652 | tf_op jit(solution)/shard_map/while
  553.7 15.5 %collective-permute-start = (f32[128,1088]{0,1:T(8,128)S(1)}, f32[128,1088]{0,1:T(8,128)S(1)}, u32[]{:S(2)}, u32[]{:S(2)}) collective-permute-start(f32[128,1088]{0,1:T(8,128)S(1)} %maximum_add_fusion.3), channel_id=1, source_target_pairs={{0,4},{4,8},{8,12},{12,16},{16,20},{20,24},{24,28},{28,32},{32,36}... | collective-permute-start | bytes 1671176 | tf_op jit(solution)/shard_map/while/body/eval_jaxpr/ppermute | solution.py:34
  555.0 14.2 %copy-start.4 = (f32[128,768]{0,1:T(8,128)}, f32[128,768]{0,1:T(8,128)S(1)}, u32[]{:S(2)}) copy-start(f32[128,768]{0,1:T(8,128)S(1)} %bitcast_add_fusion.2) | copy-start | bytes 1179652 | tf_op jit(solution)/shard_map/while
  574.7 14.7 %collective-permute-start = (f32[128,1088]{0,1:T(8,128)S(1)}, f32[128,1088]{0,1:T(8,128)S(1)}, u32[]{:S(2)}, u32[]{:S(2)}) collective-permute-start(f32[128,1088]{0,1:T(8,128)S(1)} %maximum_add_fusion.3), channel_id=1, source_target_pairs={{0,4},{4,8},{8,12},{12,16},{16,20},{20,24},{24,28},{28,32},{32,36}... | collective-permute-start | bytes 1671176 | tf_op jit(solution)/shard_map/while/body/eval_jaxpr/ppermute | solution.py:34
  575.9 13.4 %copy-start.4 = (f32[128,768]{0,1:T(8,128)}, f32[128,768]{0,1:T(8,128)S(1)}, u32[]{:S(2)}) copy-start(f32[128,768]{0,1:T(8,128)S(1)} %bitcast_add_fusion.2) | copy-start | bytes 1179652 | tf_op jit(solution)/shard_map/while
  594.7 13.8 %collective-permute-start = (f32[128,1088]{0,1:T(8,128)S(1)}, f32[128,1088]{0,1:T(8,128)S(1)}, u32[]{:S(2)}, u32[]{:S(2)}) collective-permute-start(f32[128,1088]{0,1:T(8,128)S(1)} %maximum_add_fusion.3), channel_id=1, source_target_pairs={{0,4},{4,8},{8,12},{12,16},{16,20},{20,24},{24,28},{28,32},{32,36}... | collective-permute-start | bytes 1671176 | tf_op jit(solution)/shard_map/while/body/eval_jaxpr/ppermute | solution.py:34
  614.0 13.8 %collective-permute-start = (f32[128,1088]{0,1:T(8,128)S(1)}, f32[128,1088]{0,1:T(8,128)S(1)}, u32[]{:S(2)}, u32[]{:S(2)}) collective-permute-start(f32[128,1088]{0,1:T(8,128)S(1)} %maximum_add_fusion.3), channel_id=1, source_target_pairs={{0,4},{4,8},{8,12},{12,16},{16,20},{20,24},{24,28},{28,32},{32,36}... | collective-permute-start | bytes 1671176 | tf_op jit(solution)/shard_map/while/body/eval_jaxpr/ppermute | solution.py:34
  633.2 13.8 %collective-permute-start = (f32[128,1088]{0,1:T(8,128)S(1)}, f32[128,1088]{0,1:T(8,128)S(1)}, u32[]{:S(2)}, u32[]{:S(2)}) collective-permute-start(f32[128,1088]{0,1:T(8,128)S(1)} %maximum_add_fusion.3), channel_id=1, source_target_pairs={{0,4},{4,8},{8,12},{12,16},{16,20},{20,24},{24,28},{28,32},{32,36}... | collective-permute-start | bytes 1671176 | tf_op jit(solution)/shard_map/while/body/eval_jaxpr/ppermute | solution.py:34
  652.4 13.8 %collective-permute-start = (f32[128,1088]{0,1:T(8,128)S(1)}, f32[128,1088]{0,1:T(8,128)S(1)}, u32[]{:S(2)}, u32[]{:S(2)}) collective-permute-start(f32[128,1088]{0,1:T(8,128)S(1)} %maximum_add_fusion.3), channel_id=1, source_target_pairs={{0,4},{4,8},{8,12},{12,16},{16,20},{20,24},{24,28},{28,32},{32,36}... | collective-permute-start | bytes 1671176 | tf_op jit(solution)/shard_map/while/body/eval_jaxpr/ppermute | solution.py:34
  671.7 13.8 %collective-permute-start = (f32[128,1088]{0,1:T(8,128)S(1)}, f32[128,1088]{0,1:T(8,128)S(1)}, u32[]{:S(2)}, u32[]{:S(2)}) collective-permute-start(f32[128,1088]{0,1:T(8,128)S(1)} %maximum_add_fusion.3), channel_id=1, source_target_pairs={{0,4},{4,8},{8,12},{12,16},{16,20},{20,24},{24,28},{28,32},{32,36}... | collective-permute-start | bytes 1671176 | tf_op jit(solution)/shard_map/while/body/eval_jaxpr/ppermute | solution.py:34
  690.9 13.8 %collective-permute-start = (f32[128,1088]{0,1:T(8,128)S(1)}, f32[128,1088]{0,1:T(8,128)S(1)}, u32[]{:S(2)}, u32[]{:S(2)}) collective-permute-start(f32[128,1088]{0,1:T(8,128)S(1)} %maximum_add_fusion.3), channel_id=1, source_target_pairs={{0,4},{4,8},{8,12},{12,16},{16,20},{20,24},{24,28},{28,32},{32,36}... | collective-permute-start | bytes 1671176 | tf_op jit(solution)/shard_map/while/body/eval_jaxpr/ppermute | solution.py:34
  710.1 14.6 %collective-permute-start = (f32[128,1088]{0,1:T(8,128)S(1)}, f32[128,1088]{0,1:T(8,128)S(1)}, u32[]{:S(2)}, u32[]{:S(2)}) collective-permute-start(f32[128,1088]{0,1:T(8,128)S(1)} %maximum_add_fusion.3), channel_id=1, source_target_pairs={{0,4},{4,8},{8,12},{12,16},{16,20},{20,24},{24,28},{28,32},{32,36}... | collective-permute-start | bytes 1671176 | tf_op jit(solution)/shard_map/while/body/eval_jaxpr/ppermute | solution.py:34
  711.4 13.3 %copy-start.4 = (f32[128,768]{0,1:T(8,128)}, f32[128,768]{0,1:T(8,128)S(1)}, u32[]{:S(2)}) copy-start(f32[128,768]{0,1:T(8,128)S(1)} %bitcast_add_fusion.2) | copy-start | bytes 1179652 | tf_op jit(solution)/shard_map/while
  730.1 15.8 %collective-permute-start = (f32[128,1088]{0,1:T(8,128)S(1)}, f32[128,1088]{0,1:T(8,128)S(1)}, u32[]{:S(2)}, u32[]{:S(2)}) collective-permute-start(f32[128,1088]{0,1:T(8,128)S(1)} %maximum_add_fusion.3), channel_id=1, source_target_pairs={{0,4},{4,8},{8,12},{12,16},{16,20},{20,24},{24,28},{28,32},{32,36}... | collective-permute-start | bytes 1671176 | tf_op jit(solution)/shard_map/while/body/eval_jaxpr/ppermute | solution.py:34
  731.4 14.5 %copy-start.4 = (f32[128,768]{0,1:T(8,128)}, f32[128,768]{0,1:T(8,128)S(1)}, u32[]{:S(2)}) copy-start(f32[128,768]{0,1:T(8,128)S(1)} %bitcast_add_fusion.2) | copy-start | bytes 1179652 | tf_op jit(solution)/shard_map/while
  751.3 16.9 %collective-permute-start = (f32[128,1088]{0,1:T(8,128)S(1)}, f32[128,1088]{0,1:T(8,128)S(1)}, u32[]{:S(2)}, u32[]{:S(2)}) collective-permute-start(f32[128,1088]{0,1:T(8,128)S(1)} %maximum_add_fusion.3), channel_id=1, source_target_pairs={{0,4},{4,8},{8,12},{12,16},{16,20},{20,24},{24,28},{28,32},{32,36}... | collective-permute-start | bytes 1671176 | tf_op jit(solution)/shard_map/while/body/eval_jaxpr/ppermute | solution.py:34
  752.5 15.6 %copy-start.4 = (f32[128,768]{0,1:T(8,128)}, f32[128,768]{0,1:T(8,128)S(1)}, u32[]{:S(2)}) copy-start(f32[128,768]{0,1:T(8,128)S(1)} %bitcast_add_fusion.2) | copy-start | bytes 1179652 | tf_op jit(solution)/shard_map/while
  773.6 17.3 %collective-permute-start = (f32[128,1088]{0,1:T(8,128)S(1)}, f32[128,1088]{0,1:T(8,128)S(1)}, u32[]{:S(2)}, u32[]{:S(2)}) collective-permute-start(f32[128,1088]{0,1:T(8,128)S(1)} %maximum_add_fusion.3), channel_id=1, source_target_pairs={{0,4},{4,8},{8,12},{12,16},{16,20},{20,24},{24,28},{28,32},{32,36}... | collective-permute-start | bytes 1671176 | tf_op jit(solution)/shard_map/while/body/eval_jaxpr/ppermute | solution.py:34
  774.8 16.0 %copy-start.4 = (f32[128,768]{0,1:T(8,128)}, f32[128,768]{0,1:T(8,128)S(1)}, u32[]{:S(2)}) copy-start(f32[128,768]{0,1:T(8,128)S(1)} %bitcast_add_fusion.2) | copy-start | bytes 1179652 | tf_op jit(solution)/shard_map/while
  796.2 16.5 %collective-permute-start = (f32[128,1088]{0,1:T(8,128)S(1)}, f32[128,1088]{0,1:T(8,128)S(1)}, u32[]{:S(2)}, u32[]{:S(2)}) collective-permute-start(f32[128,1088]{0,1:T(8,128)S(1)} %maximum_add_fusion.3), channel_id=1, source_target_pairs={{0,4},{4,8},{8,12},{12,16},{16,20},{20,24},{24,28},{28,32},{32,36}... | collective-permute-start | bytes 1671176 | tf_op jit(solution)/shard_map/while/body/eval_jaxpr/ppermute | solution.py:34
  797.5 15.2 %copy-start.4 = (f32[128,768]{0,1:T(8,128)}, f32[128,768]{0,1:T(8,128)S(1)}, u32[]{:S(2)}) copy-start(f32[128,768]{0,1:T(8,128)S(1)} %bitcast_add_fusion.2) | copy-start | bytes 1179652 | tf_op jit(solution)/shard_map/while
  812.7 19.9 %copy-start.10 = (bf16[128,576]{0,1:T(8,128)(2,1)S(1)}, bf16[128,576]{0,1:T(8,128)(2,1)}, u32[]{:S(2)}) copy-start(bf16[128,576]{0,1:T(8,128)(2,1)} %param.11) | copy-start | bytes 442372
  813.9 15.2 %collective-permute-start.1 = (f32[128,1088]{0,1:T(8,128)S(1)}, f32[128,1088]{0,1:T(8,128)S(1)}, u32[]{:S(2)}, u32[]{:S(2)}) collective-permute-start(f32[128,1088]{0,1:T(8,128)S(1)} %maximum_add_fusion.1), channel_id=1, source_target_pairs={{0,4},{4,8},{8,12},{12,16},{16,20},{20,24},{24,28},{28,32},{32,36}... | collective-permute-start | bytes 1671176 | tf_op jit(solution)/shard_map/ppermute | solution.py:34
  839.3 22.6 %all-to-all-start.3 = ((f32[32,1,16384]{2,1,0:T(1,128)}), f32[32,1,16384]{2,1,0:T(1,128)S(1)}, u32[]{:S(2)}, u32[]{:S(2)}) async-start(f32[32,1,16384]{2,1,0:T(1,128)} %copy.123), calls=%async_computation.3 | async-start | bytes 4194304 | tf_op jit(solution)/shard_map/all_to_all | solution.py:48
  863.1 21.7 %all-to-all-start.2 = ((f32[4,128,576]{1,2,0:T(8,128)}), f32[4,128,576]{1,2,0:T(8,128)}, u32[]{:S(2)}, u32[]{:S(2)}) async-start(f32[4,128,576]{1,2,0:T(8,128)} %broadcast_in_dim.136), calls=%async_computation.2 | async-start | bytes 2359296 | tf_op jit(solution)/shard_map/all_to_all | solution.py:22
  867.4 25.0 %copy-start.7 = (bf16[4,128,128]{1,2,0:T(8,128)(2,1)S(1)}, bf16[4,128,128]{1,2,0:T(8,128)(2,1)}, u32[]{:S(2)}) copy-start(bf16[4,128,128]{1,2,0:T(8,128)(2,1)} %copy-done.6) | copy-start | bytes 393220
  867.4 25.9 %copy-start.9 = (bf16[128,512]{0,1:T(8,128)(2,1)S(1)}, bf16[128,512]{0,1:T(8,128)(2,1)}, u32[]{:S(2)}) copy-start(bf16[128,512]{0,1:T(8,128)(2,1)} %copy.143) | copy-start | bytes 393220
  868.8 24.9 %copy-start.5 = (f32[128,768]{0,1:T(8,128)S(1)}, f32[128,768]{0,1:T(8,128)}, u32[]{:S(2)}) copy-start(f32[128,768]{0,1:T(8,128)} %get-tuple-element.503) | copy-start | bytes 1179652
  888.0 32.4 %all-to-all-start.4 = ((f32[32,1,16384]{2,1,0:T(1,128)}), f32[32,1,16384]{2,1,0:T(1,128)S(1)}, u32[]{:S(2)}, u32[]{:S(2)}) async-start(f32[32,1,16384]{2,1,0:T(1,128)} %broadcast_in_dim.137), calls=%async_computation.4 | async-start | bytes 4194304 | tf_op jit(solution)/shard_map/all_to_all | solution.py:22
  (47 other events, 345.3 us)
